TPU v7x, 128 devices: a whole 4x4x4 slice. The times are simulated.
128 devices in a mesh: rep: 1, dp: 128 (over x, y, z, core).
Axes of the slice: x: 4, y: 4, z: 4, core: 2. Of those that a mesh axis runs over, the one named last changes fastest.
Arguments:
- g_w_gate: bfloat16 [128, 2, 1024, 2816], P(('rep', 'dp'))
- g_w_up: bfloat16 [128, 2, 1024, 2816], P(('rep', 'dp'))
- g_w_down: bfloat16 [128, 2, 2816, 1024], P(('rep', 'dp'))
- w_gate: bfloat16 [2, 1024, 2816], replicated
- w_up: bfloat16 [2, 1024, 2816], replicated
- w_down: bfloat16 [2, 2816, 1024], replicated
- m_w_gate: float32 [2, 1024, 2816], P(None, 'dp')
- m_w_up: float32 [2, 1024, 2816], P(None, 'dp')
- m_w_down: float32 [2, 2816, 1024], P(None, 'dp')
- v_w_gate: float32 [2, 1024, 2816], P(None, 'dp')
- v_w_up: float32 [2, 1024, 2816], P(None, 'dp')
- v_w_down: float32 [2, 2816, 1024], P(None, 'dp')
Outputs:
- output 1: bfloat16 [2, 1024, 2816], P('rep')
- output 2: bfloat16 [2, 1024, 2816], P('rep')
- output 3: bfloat16 [2, 2816, 1024], P('rep')
- output 4: float32 [2, 1024, 2816], P('rep', 'dp')
- output 5: float32 [2, 1024, 2816], P('rep', 'dp')
- output 6: float32 [2, 2816, 1024], P('rep', 'dp')
- output 7: float32 [2, 1024, 2816], P('rep', 'dp')
- output 8: float32 [2, 1024, 2816], P('rep', 'dp')
- output 9: float32 [2, 2816, 1024], P('rep', 'dp')
All inputs are finite; a program needn't handle non-finite values.
Results may differ from a plain program's by a relative error of at most 0.022.
Values are sent between devices in bfloat16 or wider.
A program may use at most 1.5 GiB of HBM per device.

v0:
```python
import jax
import jax.numpy as jnp
from jax import lax
from jax.sharding import PartitionSpec as P


def adamw(w, m, v, g):
    m = 0.9 * m + 0.1 * g
    v = 0.95 * v + 0.05 * g * g
    step = m * lax.rsqrt(v + 1e-8) + 0.1 * w
    return (w - 0.02 * step).astype(jnp.bfloat16), m, v


def clipped(gradients, sum_of_squares, count):
    factor = jnp.minimum(1.0, 0.5 * lax.rsqrt(sum_of_squares / count + 1e-30))
    return [g * factor for g in gradients]


def solution(mesh):
    def step(*arrays):
        terms, weights, m, v = (arrays[i : i + 3] for i in (0, 3, 6, 9))
        gradients = [lax.psum_scatter(t[0], "dp", scatter_dimension=1, tiled=True).astype(jnp.float32) for t in terms]
        squares = lax.psum(sum(jnp.sum(g * g) for g in gradients), "dp")
        gradients = clipped(gradients, squares, lax.psum(1, "dp") * sum(g.size for g in gradients))
        me = lax.axis_index("dp")
        own = [lax.dynamic_slice_in_dim(w, me * one.shape[1], one.shape[1], 1).astype(jnp.float32) for w, one in zip(weights, m, strict=True)]
        new = [adamw(w, m, v, g) for w, m, v, g in zip(own, m, v, gradients, strict=True)]
        whole = [lax.all_gather(one[0], "dp", axis=1, tiled=True) for one in new]
        return (*whole, *(one[1] for one in new), *(one[2] for one in new))

    all_of, cut = P(None, None, None), P(None, "dp", None)
    return jax.shard_map(
        step,
        mesh=mesh,
        in_specs=(P(("rep", "dp"), None, None, None),) * 3 + (all_of,) * 3 + (cut,) * 6,
        out_specs=(P("rep", None, None),) * 3 + (P("rep", "dp", None),) * 6,
        check_vma=False,
    )
```

profile of v0, /device:TPU:1, one launch (start us, length us, event | category | flops | bytes accessed | tf_op | source)
XLA Modules:
  0.0 1832.6 jit_solution(782822718342675091)
XLA Ops:
  7.2 0.0 all-reduce.3.cloned.1.call-start
  7.2 21.9 %copy.46 = bf16[1,2,2816,1024]{3,1,2,0:T(2,128)(2,1)} copy(bf16[1,2,2816,1024]{3,2,1,0:T(8,128)(2,1)} %param.14) | data formatting | bytes 23068672 | tf_op args[2]
  29.1 0.0 all-reduce.3.cloned.1.call-update
  29.1 0.0 reduce-scatter.7.cloned.1.call-start
  29.1 21.2 %copy.27 = bf16[2,1024,2816]{2,0,1:T(2,128)(2,1)S(1)} copy(bf16[2,1024,2816]{2,1,0:T(8,128)(2,1)} %bitcast.18) | data formatting | bytes 23068672
  50.3 5.8 copy.32
  56.2 0.0 reduce-scatter.7.cloned.1.call-update
  56.2 0.0 reduce-scatter.9.cloned.1.call-start
  56.3 21.2 %copy.29 = bf16[2,1024,2816]{2,0,1:T(2,128)(2,1)S(1)} copy(bf16[2,1024,2816]{2,1,0:T(8,128)(2,1)} %bitcast.19) | data formatting | bytes 23068672
  77.4 5.8 copy.33
  83.3 0.0 copy-start.1
  83.3 0.0 copy-start.2
  83.3 0.0 copy-start.3
  83.3 0.0 copy-start.4
  83.3 0.0 copy-start.5
  83.3 0.0 copy-start.6
  83.3 0.0 reduce-scatter.9.cloned.1.call-update
  83.4 0.0 all-gather.8.cloned.1.call-start
  83.4 114.8 %all-reduce.3.cloned.1.call-done = bf16[2,2816,1024]{2,0,1:T(2,128)(2,1)} async-done(((bf16[2,2816,1024]{2,0,1:T(2,128)(2,1)}), bf16[2,2816,1024]{2,0,1:T(2,128)(2,1)}) %all-reduce.3.cloned.1.call-update) | async-done | bytes 11534352
  198.2 1.7 fusion.11
  199.9 655.5 %reduce-scatter.7.cloned.1.call-done = bf16[8,5632]{1,0:T(8,128)(2,1)} async-done(((bf16[1024,5632]{1,0:T(8,128)(2,1)}), bf16[8,5632]{1,0:T(8,128)(2,1)}) %reduce-scatter.7.cloned.1.call-update) | async-done | bytes 90128
  855.4 0.9 reshape.19
  856.3 658.3 %reduce-scatter.9.cloned.1.call-done = bf16[8,5632]{1,0:T(8,128)(2,1)} async-done(((bf16[1024,5632]{1,0:T(8,128)(2,1)}), bf16[8,5632]{1,0:T(8,128)(2,1)}) %reduce-scatter.9.cloned.1.call-update) | async-done | bytes 90128
  1514.6 0.9 reshape.21
  1515.5 0.7 fusion.9
  1518.2 0.9 constant_dynamic-slice_fusion
  1519.1 69.3 %psum.7 = f32[]{:T(128)} all-reduce(f32[]{:T(128)S(6)} %add.65), channel_id=1, replica_groups=mesh['rep'=1,'dp'=128] {'dp'}, use_global_device_ids=true, to_apply=%region_6.0 | all-reduce | flops 1 | bytes 8 | tf_op jit(solution)/shard_map/psum | solution.py:23
  1589.0 0.0 copy-done.1
  1589.1 0.0 copy-done.2
  1589.1 2.1 fusion.20
  1591.2 0.0 all-gather.8.cloned.1.call-update
  1591.2 0.0 all-gather.4.cloned.1.call-start
  1591.3 0.0 copy-done.3
  1591.3 0.0 copy-done.4
  1591.3 1.7 fusion.8
  1593.0 0.0 all-gather.4.cloned.1.call-update
  1593.0 0.0 all-gather.6.cloned.1.call-start
  1593.0 0.0 copy-done.5
  1593.1 0.0 copy-done.6
  1593.1 1.7 fusion.14
  1594.8 0.0 all-gather.6.cloned.1.call-update
  1594.8 65.3 %all-gather.8.cloned.1.call-done = bf16[2,2816,1024]{2,0,1:T(2,128)(2,1)} async-done(((bf16[2,22,1024]{2,0,1:T(2,128)(2,1)}), bf16[2,2816,1024]{2,0,1:T(2,128)(2,1)}) %all-gather.8.cloned.1.call-update) | async-done | bytes 11534352 | tf_op jit(solution)/shard_map/all_gather | solution.py:28
  1660.1 11.8 copy.26
  1671.9 62.9 %all-gather.4.cloned.1.call-done = bf16[2,1024,2816]{2,1,0:T(8,128)(2,1)} async-done(((bf16[2,8,2816]{2,1,0:T(8,128)(2,1)}), bf16[2,1024,2816]{2,1,0:T(8,128)(2,1)}) %all-gather.4.cloned.1.call-update) | async-done | bytes 11534352 | tf_op jit(solution)/shard_map/all_gather | solution.py:28
  1734.8 74.6 %all-gather.6.cloned.1.call-done = bf16[2,1024,2816]{2,1,0:T(8,128)(2,1)} async-done(((bf16[2,8,2816]{2,1,0:T(8,128)(2,1)}), bf16[2,1024,2816]{2,1,0:T(8,128)(2,1)}) %all-gather.6.cloned.1.call-update) | async-done | bytes 11534352 | tf_op jit(solution)/shard_map/all_gather | solution.py:28
  1809.4 10.4 copy.50
  1819.8 1.5 copy-done
  1821.4 4.4 copy.51
  (1 shorter events, 0.0 us)
Async XLA Ops:
  7.2 191.1 %all-reduce.3.cloned.1.call-start = ((), (), s32[]{:S(2)}) async-start(), calls=%async_computation.7 | async-start | bytes 23068672
  29.1 826.3 %reduce-scatter.7.cloned.1.call-start = ((), (), s32[]{:S(2)}) async-start(), calls=%async_computation.5 | async-start | bytes 11624448
  56.2 1458.4 %reduce-scatter.9.cloned.1.call-start = ((), (), s32[]{:S(2)}) async-start(), calls=%async_computation.6 | async-start | bytes 11624448
  83.3 1505.8 %copy-start.1 = (f32[2,22,1024]{2,0,1:T(2,128)S(1)}, f32[2,22,1024]{2,0,1:T(2,128)}, u32[]{:S(2)}) copy-start(f32[2,22,1024]{2,0,1:T(2,128)} %param.23) | copy-start | bytes 540676
  83.3 1505.8 %copy-start.2 = (f32[2,22,1024]{2,0,1:T(2,128)S(1)}, f32[2,22,1024]{2,0,1:T(2,128)}, u32[]{:S(2)}) copy-start(f32[2,22,1024]{2,0,1:T(2,128)} %param.20) | copy-start | bytes 540676
  83.3 1508.0 %copy-start.3 = (f32[2,8,2816]{2,1,0:T(8,128)S(1)}, f32[2,8,2816]{2,1,0:T(8,128)}, u32[]{:S(2)}) copy-start(f32[2,8,2816]{2,1,0:T(8,128)} %param.21) | copy-start | bytes 540676
  83.3 1508.0 %copy-start.4 = (f32[2,8,2816]{2,1,0:T(8,128)S(1)}, f32[2,8,2816]{2,1,0:T(8,128)}, u32[]{:S(2)}) copy-start(f32[2,8,2816]{2,1,0:T(8,128)} %param.18) | copy-start | bytes 540676
  83.3 1509.7 %copy-start.5 = (f32[2,8,2816]{2,1,0:T(8,128)S(1)}, f32[2,8,2816]{2,1,0:T(8,128)}, u32[]{:S(2)}) copy-start(f32[2,8,2816]{2,1,0:T(8,128)} %param.22) | copy-start | bytes 540676
  83.3 1509.7 %copy-start.6 = (f32[2,8,2816]{2,1,0:T(8,128)S(1)}, f32[2,8,2816]{2,1,0:T(8,128)}, u32[]{:S(2)}) copy-start(f32[2,8,2816]{2,1,0:T(8,128)} %param.19) | copy-start | bytes 540676
  83.4 1576.8 %all-gather.8.cloned.1.call-start = ((), (), s32[]{:S(2)}) async-start(), calls=%async_computation.4 | async-start | bytes 11624448 | tf_op jit(solution)/shard_map/all_gather | solution.py:28
  1591.2 143.6 %all-gather.4.cloned.1.call-start = ((), (), s32[]{:S(2)}) async-start(), calls=%async_computation.2 | async-start | bytes 11624448 | tf_op jit(solution)/shard_map/all_gather | solution.py:28
  1593.0 216.4 %all-gather.6.cloned.1.call-start = ((), (), s32[]{:S(2)}) async-start(), calls=%async_computation.3 | async-start | bytes 11624448 | tf_op jit(solution)/shard_map/all_gather | solution.py:28
  1809.4 11.9 copy-start
Sparse Core Ops, SparseCore 0:
  29.2 168.9 all-reduce.2
  201.2 654.1 reduce-scatter.6
  858.4 656.1 reduce-scatter.8
  1591.3 68.7 all-gather.7
  1663.8 70.9 all-gather.3
  1738.5 70.9 all-gather.5
where the time goes:
time: 1830 us
  waiting for transfers between devices  1630 us (89%)
  local copies, waits for them, and re-layouts  107 us (6%)
  blocking collectives  69.3 us (4%)
    unnamed x9, waiting for transfers between devices  1430 us
    all_gather x3, waiting for transfers between devices, step(): whole = [lax.all_gather(one[0], 'dp', axis=1, tiled=True) for one in new]  203 us
    unnamed x24, local copies, waits for them, and re-layouts  106 us
    psum x1, blocking collectives, step(): squares = lax.psum(sum((jnp.sum(g * g) for g in gradients)), 'dp')  69.3 us
  transfers between devices with their start and end apart: 6, of which 6 were waited for; matrix products, arithmetic and copies ran while one was open for 4% of the time, Pallas kernels for 0%

commit v1 on v0

v1 whole, which is shorter than its diff:
```python
import functools

import jax
import jax.numpy as jnp
from jax import lax
from jax.experimental import pallas as pl
from jax.experimental.pallas import tpu as pltpu
from jax.sharding import PartitionSpec as P

MESH = pl.DeviceIdType.MESH
F32, BF16 = jnp.float32, jnp.bfloat16
AXES = ((0, 1, 2), (1, 2, 0), (2, 0, 1))
LAYERS = 2
EACH, SIDES, PLACES, OTHERS, LANDED = range(3), range(2), range(4), range(1, 4), range(2, 6)
AHEAD, BEHIND = (1, 3), (3, 1)


def order(j):
    return lax.rem(2 + j + (j // 2) * (2 * j - 3), 4)


def loop(body, n=4):
    lax.fori_loop(0, n, lambda j, c: (body(j), c)[1], 0)


def f32(x):
    return x.astype(F32)


def step_kernel(
    count, gg, gu, gd, wg, wu, wd, mg, mu, md, vg, vu, vd,
    Wg, Wu, Wd, mg2, mu2, md2, vg2, vu2, vd2,
    R1g, R1u, R1d, R2g, R2u, R2d, Q1g, Q1u, Q1d, Q2g, Q2u, Q2d, P1g, P1u, P1d, P2g, P2u, P2d,
    own_g, own_u, own_d, quad_g, rows, new_rows, cols, norms,
    load_sem, own_sem, d2d_s, d2d_r, a_s, a_r, b_s, b_r, c_s, c_r, x_s, x_r, n_s, n_r,
):
    g_in, W, w_in = (gg, gu, gd), (Wg, Wu, Wd), (wg, wu, wd)
    R1, R2, Q1, Q2, P1, P2 = (R1g, R1u, R1d), (R2g, R2u, R2d), (Q1g, Q1u, Q1d), (Q2g, Q2u, Q2d), (P1g, P1u, P1d), (P2g, P2u, P2d)
    quarter = cols.shape[-1]
    me = lax.axis_index("dp")
    k = lax.rem(me, 2)
    pos = (me // 32, lax.rem(me // 8, 4), lax.rem(me // 2, 4))
    q = lax.rem(me, 4)

    def device(p, core):
        return ((p[0] * 4 + p[1]) * 4 + p[2]) * 2 + core

    def near(axis, by):
        return device([lax.rem(c + by, 4) if n == axis else c for n, c in enumerate(pos)], k)

    partner = device(pos, 1 - k)
    quad = [me - q + lax.rem(q + by, 4) for by in OTHERS]

    def copy(src, dst, send, recv, to):
        return pltpu.make_async_remote_copy(src_ref=src, dst_ref=dst, send_sem=send, recv_sem=recv, device_id={"dp": to}, device_id_type=MESH)

    def at(i, l, a, b, c, core):
        place = dict(zip(AXES[i], (a, b, c)))
        return W[i].at[l, place[0], place[1], place[2], core]

    ALL = slice(None)
    home = [[pos[n] for n in AXES[i]] for i in EACH]

    def rel(i, which, by):
        return lax.rem(home[i][which] + by, 4)

    def source(i, a, b, core):
        if i == 0:
            return gg.at[:, a, b, :, core]
        if i == 1:
            return gu.at[:, :, a, b, core]
        columns = pl.ds(pl.multiple_of(lax.rem(a, 2) * (2 * quarter) + core * quarter, quarter), quarter)
        return gd.at[:, b, :, a // 2, :, :, columns]

    def load(i, ra, rb):
        a, b = rel(i, 0, ra), rel(i, 1, rb)
        return pltpu.make_async_copy(source(i, a, b, k), at(i, ALL, a, b, ALL, k), load_sem.at[i, ra, rb])

    def trade(i, ra, rb):
        a, b = rel(i, 0, ra), rel(i, 1, rb)
        return copy(source(i, a, b, 1 - k), at(i, ALL, a, b, ALL, k), d2d_s.at[i, ra, rb], d2d_r.at[i, ra, rb], partner)

    def traded(i, ra, rb):
        a, b = rel(i, 0, ra), rel(i, 1, rb)
        load(i, ra, rb).wait()
        copy(at(i, ALL, a, b, ALL, 1 - k), at(i, ALL, a, b, ALL, 1 - k), d2d_s.at[i, ra, rb], d2d_r.at[i, ra, rb], partner).wait_recv()

    across = me - q + (2 - 2 * (q // 2)) + (1 - k)
    peers = [partner, across] + [near(axis, by) for axis in EACH for by in OTHERS]
    barrier = pltpu.get_barrier_semaphore()
    for peer in peers:
        pl.semaphore_signal(barrier, inc=1, device_id={"dp": peer}, device_id_type=MESH)

    for ras in ((2,), (1, 3), (0,)):
        def start_loads(j, ras=ras):
            for ra in ras:
                for i in EACH:
                    load(i, ra, order(j)).start()
        if ras == (2,):
            loop(start_loads)
            pl.semaphore_wait(barrier, len(peers))
        else:
            loop(start_loads)
        def start_trades(j, ras=ras):
            for ra in ras:
                for i in EACH:
                    trade(i, ra, order(j)).start()
        loop(start_trades)
    own = [
        pltpu.make_async_copy(wg.at[:, pos[0], pos[1], pos[2], k], own_g, own_sem.at[0]),
        pltpu.make_async_copy(wu.at[:, pos[0], pos[1], pos[2], k], own_u, own_sem.at[1]),
        pltpu.make_async_copy(wd.at[:, pos[0], pos[1], pos[2] // 2], own_d, own_sem.at[2]),
    ]
    for n, (moment, there) in enumerate(zip((mg, mu, md, vg, vu, vd), (mg2, mu2, md2, vg2, vu2, vd2))):
        own.append(pltpu.make_async_copy(moment, there, own_sem.at[3 + n]))
    for one in own:
        one.start()

    def sum0(i, l, a, b, c):
        return f32(at(i, l, a, b, c, k)[...]) + f32(at(i, l, a, b, c, 1 - k)[...])

    def sum1(i, l, b, c):
        return sum0(i, l, home[i][0], b, c) + f32(R2[i][0, l, b, c]) + f32(R2[i][1, l, b, c])

    def sum2(i, l, c):
        return sum1(i, l, home[i][1], c) + f32(Q2[i][0, l, c]) + f32(Q2[i][1, l, c])

    def sum3(i, l):
        return sum2(i, l, home[i][2]) + f32(P2[i][0, l]) + f32(P2[i][1, l])

    def hop_a(i, kind, rb):
        d, b = kind % 2, rel(i, 1, rb)
        to = near(AXES[i][0], AHEAD[d])
        if kind < 2:
            src, dst = at(i, d, rel(i, 0, 2), b, ALL, k), R1[i].at[d, b]
        elif kind < 4:
            src, dst = at(i, 1 - d, rel(i, 0, AHEAD[d]), b, ALL, k), R2[i].at[d, 1 - d, b]
        else:
            src, dst = R1[i].at[d, b], R2[i].at[d, d, b]
        return copy(src, dst, a_s.at[i, kind, rb], a_r.at[i, kind, rb], to)

    def hop_b(i, kind):
        d = kind % 2
        to = near(AXES[i][1], AHEAD[d])
        if kind < 2:
            src, dst = R2[i].at[0, d, rel(i, 1, 2)], Q1[i].at[d]
        elif kind < 4:
            src, dst = R2[i].at[0, 1 - d, rel(i, 1, AHEAD[d])], Q2[i].at[d, 1 - d]
        else:
            src, dst = Q1[i].at[d], Q2[i].at[d, d]
        return copy(src, dst, b_s.at[i, kind], b_r.at[i, kind], to)

    def hop_c(i, kind):
        d = kind % 2
        to = near(AXES[i][2], AHEAD[d])
        if kind < 2:
            src, dst = Q2[i].at[0, d, rel(i, 2, 2)], P1[i].at[d]
        elif kind < 4:
            src, dst = Q2[i].at[0, 1 - d, rel(i, 2, AHEAD[d])], P2[i].at[d, 1 - d]
        else:
            src, dst = P1[i].at[d], P2[i].at[d, d]
        return copy(src, dst, c_s.at[i, kind], c_r.at[i, kind], to)

    def farthest(j):
        rb = order(j)
        for i in EACH:
            traded(i, 2, rb)
            a, b = rel(i, 0, 2), rel(i, 1, rb)

            def add(t):
                at(i, t // 4, a, b, lax.rem(t, 4), k)[...] = sum0(i, t // 4, a, b, lax.rem(t, 4)).astype(BF16)

            loop(add, 8)
            hop_a(i, 0, rb).start()
            hop_a(i, 1, rb).start()

    loop(farthest)

    def plain(j):
        rb = order(j)
        for i in EACH:
            for d in SIDES:
                ra = AHEAD[d]
                traded(i, ra, rb)
                a, b = rel(i, 0, ra), rel(i, 1, rb)

                def add(c):
                    at(i, 1 - d, a, b, c, k)[...] = sum0(i, 1 - d, a, b, c).astype(BF16)

                loop(add)
                hop_a(i, 2 + d, rb).start()

    loop(plain)

    def onward(j):
        rb = order(j)
        for i in EACH:
            for d in SIDES:
                hop_a(i, d, rb).wait_recv()
                a, b = rel(i, 0, AHEAD[d]), rel(i, 1, rb)

                def add(c):
                    R1[i][d, b, c] = (f32(R1[i][d, b, c]) + sum0(i, d, a, b, c)).astype(BF16)

                loop(add)
                hop_a(i, 4 + d, rb).start()

    loop(onward)

    def arrived_a(i, rb):
        traded(i, 0, rb)
        for kind in LANDED:
            hop_a(i, kind, rb).wait_recv()

    def settle_a(i, l, rb):
        b = rel(i, 1, rb)

        def add(c):
            R2[i][0, l, b, c] = sum1(i, l, b, c).astype(BF16)

        loop(add)

    for i in EACH:
        arrived_a(i, 2)
        for d in SIDES:
            settle_a(i, d, 2)
            hop_b(i, d).start()
    for rb, d in ((3, 1), (1, 0)):
        for i in EACH:
            arrived_a(i, rb)
            settle_a(i, 1 - d, rb)
            hop_b(i, 2 + d).start()
    for i in EACH:
        for d in SIDES:
            hop_b(i, d).wait_recv()
            b = rel(i, 1, AHEAD[d])

            def add(c, i=i, d=d, b=b):
                Q1[i][d, c] = (f32(Q1[i][d, c]) + sum1(i, d, b, c)).astype(BF16)

            loop(add)
            hop_b(i, 4 + d).start()

    for i in EACH:
        arrived_a(i, 0)
    for i in EACH:
        for kind in LANDED:
            hop_b(i, kind).wait_recv()
        for d in SIDES:
            c = rel(i, 2, 2)
            Q2[i][0, d, c] = sum2(i, d, c).astype(BF16)
            hop_c(i, d).start()
        for d in SIDES:
            c = rel(i, 2, AHEAD[d])
            Q2[i][0, 1 - d, c] = sum2(i, 1 - d, c).astype(BF16)
            hop_c(i, 2 + d).start()
    for i in EACH:
        for d in SIDES:
            hop_c(i, d).wait_recv()
            P1[i][d] = (f32(P1[i][d]) + sum2(i, d, rel(i, 2, AHEAD[d]))).astype(BF16)
            hop_c(i, 4 + d).start()
    squares = jnp.zeros((8, 128), F32)
    for i in (2, 0, 1):
        for kind in LANDED:
            hop_c(i, kind).wait_recv()
        for l in SIDES:
            total = sum3(i, l).astype(BF16)
            if i == 2:
                quad_g[q, l] = total
            else:
                P2[i][0, l] = total
            s = f32(total)
            s = s * s
            if i == 2:
                s = jnp.sum(s, axis=0)
            for lane in range(0, s.shape[-1], 128):
                squares = squares + s[:, lane : lane + 128]
        if i == 2:
            for n in EACH:
                copy(quad_g.at[q], quad_g.at[q], x_s.at[n], x_r.at[n], quad[n]).start()
    norms[0, 0] = squares

    def drain(j):
        for i in EACH:
            for kind in range(6):
                hop_a(i, kind, j).wait_send()
            for ra in PLACES:
                trade(i, ra, j).wait_send()

    loop(drain)
    for i in EACH:
        for kind in range(6):
            hop_b(i, kind).wait_send()
            hop_c(i, kind).wait_send()

    first = copy(norms.at[0, 0], norms.at[0, 1], n_s.at[0, 1], n_r.at[0, 1], partner)
    first.start()
    first.wait()
    norms[1, 0] = norms[0, 0] + norms[0, 1]
    for turn, axis in ((1, 2), (2, 1), (3, 0)):
        hops = [copy(norms.at[turn, 0], norms.at[turn, by], n_s.at[turn, by], n_r.at[turn, by], near(axis, by)) for by in OTHERS]
        for hop in hops:
            hop.start()
        for hop in hops:
            hop.wait()
        norms[turn + 1, 0] = (norms[turn, 0] + norms[turn, 1]) + (norms[turn, 2] + norms[turn, 3])
    squares = norms[4, 0]
    squares = jnp.sum(jnp.sum(squares, axis=1, keepdims=True), axis=0, keepdims=True)
    factor = jnp.minimum(1.0, 0.5 * lax.rsqrt(squares / count + 1e-30))

    def adamw(w, m, v, g):
        g = g * factor
        m = 0.9 * m + 0.1 * g
        v = 0.95 * v + 0.05 * g * g
        step = m * lax.rsqrt(v + 1e-8) + 0.1 * w
        return (w - 0.02 * step).astype(BF16), m, v

    for one in own:
        one.wait()
    for n in EACH:
        copy(quad_g.at[q], quad_g.at[q], x_s.at[n], x_r.at[n], quad[n]).wait_send()
        theirs = quad_g.at[lax.rem(q + n + 1, 4)]
        copy(theirs, theirs, x_s.at[2 - n], x_r.at[2 - n], quad[n]).wait_recv()
    n_rows = md.shape[0]
    for l in SIDES:
        for n in PLACES:
            rows[0, :, n * quarter : (n + 1) * quarter] = f32(quad_g[n, l]).reshape(4 * n_rows, quarter)
        rows[1] = f32(own_d[l]).reshape(4 * n_rows, 4 * quarter)
        for n in PLACES:

            @pl.when(q == n)
            def _():
                mine = slice(n * n_rows, (n + 1) * n_rows)
                new, m, v = adamw(rows[1, mine, :], md2[:, l, :], vd2[:, l, :], rows[0, mine, :])
                new_rows[l] = new
                md2[:, l, :] = m
                vd2[:, l, :] = v
                cols[n, l] = new[:, n * quarter : (n + 1) * quarter]

    def piece(n):
        to = lax.rem(q + n + 1, 4)
        return new_rows.at[:, :, pl.ds(pl.multiple_of(to * quarter, quarter), quarter)]

    for n in EACH:
        copy(piece(n), cols.at[q], x_s.at[3 + n], x_r.at[3 + n], quad[n]).start()

    for i, own_w, m_ref, v_ref in ((0, own_g, mg2, vg2), (1, own_u, mu2, vu2)):
        for l in SIDES:
            new, m_ref[l], v_ref[l] = adamw(f32(own_w[l]), m_ref[l], v_ref[l], f32(P2[i][0, l]))
            at(i, l, *home[i], k)[...] = new

    def back_c(i, kind):
        d = kind % 2
        a, b, c = home[i]
        if kind < 2:
            ref = at(i, ALL, a, b, c, k)
        else:
            ref = at(i, d, a, b, rel(i, 2, BEHIND[d]), k)
        return copy(ref, ref, c_s.at[i, kind], c_r.at[i, kind], near(AXES[i][2], AHEAD[d]))

    def came_c(i, kind):
        d = kind % 2
        a, b, _ = home[i]
        ref = at(i, ALL, a, b, rel(i, 2, BEHIND[d]), k) if kind < 2 else at(i, d, a, b, rel(i, 2, 2), k)
        copy(ref, ref, c_s.at[i, kind], c_r.at[i, kind], partner).wait_recv()

    def back_b(i, kind):
        d = kind % 2
        a, b, _ = home[i]
        if kind < 2:
            ref = at(i, ALL, a, b, ALL, k)
        else:
            ref = at(i, d, a, rel(i, 1, BEHIND[d]), ALL, k)
        return copy(ref, ref, b_s.at[i, kind], b_r.at[i, kind], near(AXES[i][1], AHEAD[d]))

    def came_b(i, kind):
        d = kind % 2
        ref = at(i, ALL, home[i][0], rel(i, 1, BEHIND[d]), ALL, k) if kind < 2 else at(i, d, home[i][0], rel(i, 1, 2), ALL, k)
        copy(ref, ref, b_s.at[i, kind], b_r.at[i, kind], partner).wait_recv()

    def back_a(i, kind, rb):
        d, b = kind % 2, rel(i, 1, rb)
        if kind < 2:
            ref = at(i, ALL, home[i][0], b, ALL, k)
        else:
            ref = at(i, d, rel(i, 0, BEHIND[d]), b, ALL, k)
        return copy(ref, ref, a_s.at[i, kind, rb], a_r.at[i, kind, rb], near(AXES[i][0], AHEAD[d]))

    def came_a(i, kind, rb):
        d, b = kind % 2, rel(i, 1, rb)
        ref = at(i, ALL, rel(i, 0, BEHIND[d]), b, ALL, k) if kind < 2 else at(i, d, rel(i, 0, 2), b, ALL, k)
        copy(ref, ref, a_s.at[i, kind, rb], a_r.at[i, kind, rb], partner).wait_recv()

    def share(i, ra, rb):
        ref = at(i, ALL, rel(i, 0, ra), rel(i, 1, rb), ALL, k)
        return copy(ref, ref, d2d_s.at[i, ra, rb], d2d_r.at[i, ra, rb], partner)

    def shared(i, ra, rb):
        ref = at(i, ALL, rel(i, 0, ra), rel(i, 1, rb), ALL, 1 - k)
        copy(ref, ref, d2d_s.at[i, ra, rb], d2d_r.at[i, ra, rb], partner).wait_recv()

    for i in (0, 1):
        for kind in SIDES:
            back_c(i, kind).start()
    for n in EACH:
        copy(piece(n), cols.at[q], x_s.at[3 + n], x_r.at[3 + n], quad[n]).wait_send()
        theirs = cols.at[lax.rem(q + n + 1, 4)]
        copy(theirs, theirs, x_s.at[5 - n], x_r.at[5 - n], quad[n]).wait_recv()
    for l in SIDES:
        for n in PLACES:
            rows[0, n * n_rows : (n + 1) * n_rows, 0:quarter] = f32(cols[n, l])
        at(2, l, *home[2], k)[...] = rows[0, :, 0:quarter].reshape(n_rows // 2, 8, quarter).astype(BF16)
    for kind in SIDES:
        back_c(2, kind).start()
    for i in EACH:
        for d in SIDES:
            came_c(i, d)
            back_c(i, 2 + d).start()
    for i in EACH:
        for d in SIDES:
            came_c(i, 2 + d)
        for kind in SIDES:
            back_b(i, kind).start()
    for i in EACH:
        for kind in SIDES:
            back_a(i, kind, 0).start()
        share(i, 0, 0).start()
    for i in EACH:
        for d in SIDES:
            came_b(i, d)
            back_b(i, 2 + d).start()
    for i in EACH:
        for rb in (3, 1):
            for kind in SIDES:
                back_a(i, kind, rb).start()
            share(i, 0, rb).start()
    for i in EACH:
        for d in SIDES:
            came_b(i, 2 + d)
        for kind in SIDES:
            back_a(i, kind, 2).start()
        share(i, 0, 2).start()

    def pass_on(j):
        rb = lax.rem(order(j) + 2, 4)
        for i in EACH:
            for d in SIDES:
                came_a(i, d, rb)
                back_a(i, 2 + d, rb).start()
                share(i, BEHIND[d], rb).start()

    loop(pass_on)

    def last(j):
        rb = lax.rem(order(j) + 2, 4)
        for i in EACH:
            for d in SIDES:
                came_a(i, 2 + d, rb)
            share(i, 2, rb).start()

    loop(last)

    def finish(j):
        for i in EACH:
            for ra in PLACES:
                shared(i, ra, j)
                share(i, ra, j).wait_send()
            for kind in PLACES:
                back_a(i, kind, j).wait_send()

    loop(finish)
    for i in EACH:
        for kind in PLACES:
            back_b(i, kind).wait_send()
            back_c(i, kind).wait_send()


def write_kernel(Wg, Wu, Wd, *refs):
    small_in, (og, ou, od), outs, sems = refs[:6], refs[6:9], refs[9:15], refs[15]
    quarter = Wd.shape[-1]
    copies = [pltpu.make_async_copy(Wg, og, sems.at[14]), pltpu.make_async_copy(Wu, ou, sems.at[15])]
    for n in PLACES:
        for zh in SIDES:
            copies.append(
                pltpu.make_async_copy(Wd.at[:, :, :, 2 * zh + n // 2, n % 2], od.at[:, :, :, zh, :, :, n * quarter : (n + 1) * quarter], sems.at[2 * n + zh])
            )
    for n in range(6):
        copies.append(pltpu.make_async_copy(small_in[n], outs[n], sems.at[8 + n]))
    for one in copies:
        one.start()
    for one in copies:
        one.wait()


def solution(mesh):
    def step(*arrays):
        terms, weights, m, v = (arrays[i : i + 3] for i in (0, 3, 6, 9))
        wide, tall = weights[0].shape[2], weights[2].shape[2]
        n_rows = m[2].shape[1]
        m, v = ([jnp.swapaxes(one, 0, 1) if n == 2 else one for n, one in enumerate(some)] for some in (m, v))
        whole = (LAYERS, 4, 4, 4, 2, 8, wide)
        whole_d = (LAYERS, 4, 4, 2, n_rows // 2, 8, tall)
        shapes = (whole, whole, whole_d)
        quarter = tall // 4
        units = ((8, wide), (8, wide), (n_rows // 2, 8, quarter))
        g = [t[0].reshape(s) for t, s in zip(terms, shapes)]
        w = [t.reshape(s) for t, s in zip(weights, shapes)]
        count = float(sum(one.size for one in weights))
        blocks = [pltpu.VMEM((LAYERS, 4, 4, 4, 2, *u), BF16) for u in units]
        moments = [pltpu.VMEM(one.shape, F32) for one in (*m, *v)]
        hbm, vmem = pl.BlockSpec(memory_space=pltpu.HBM), pl.BlockSpec(memory_space=pltpu.VMEM)
        dma = pltpu.SemaphoreType.DMA
        results = pl.pallas_call(
            functools.partial(step_kernel, count),
            out_shape=blocks + moments,
            in_specs=[hbm] * 12,
            out_specs=[vmem] * 9,
            scratch_shapes=[
                *[pltpu.VMEM((2, 4, 4, *u), BF16) for u in units],
                *[pltpu.VMEM((2, LAYERS, 4, 4, *u), BF16) for u in units],
                *[pltpu.VMEM((2, 4, *u), BF16) for u in units],
                *[pltpu.VMEM((2, LAYERS, 4, *u), BF16) for u in units],
                *[pltpu.VMEM((2, *u), BF16) for u in units],
                *[pltpu.VMEM((2, LAYERS, *u), BF16) for u in units],
                pltpu.VMEM((LAYERS, 8, wide), BF16),
                pltpu.VMEM((LAYERS, 8, wide), BF16),
                pltpu.VMEM((LAYERS, n_rows // 2, 8, tall), BF16),
                pltpu.VMEM((4, LAYERS, *units[2]), BF16),
                pltpu.VMEM((2, 4 * n_rows, tall), F32),
                pltpu.VMEM((LAYERS, n_rows, tall), BF16),
                pltpu.VMEM((4, LAYERS, n_rows, quarter), BF16),
                pltpu.VMEM((5, 4, 8, 128), F32),
                dma((3, 4, 4)), dma((9,)), dma((3, 4, 4)), dma((3, 4, 4)),
                dma((3, 6, 4)), dma((3, 6, 4)), dma((3, 6)), dma((3, 6)), dma((3, 6)), dma((3, 6)),
                dma((6,)), dma((6,)), dma((4, 4)), dma((4, 4)),
            ],
            compiler_params=pltpu.CompilerParams(collective_id=0, has_side_effects=True, vmem_limit_bytes=26600000),
            name="step",
        )(*g, *w, *m, *v)
        outs = [jax.ShapeDtypeStruct(s, BF16) for s in shapes] + [jax.ShapeDtypeStruct(one.shape, F32) for one in (*m, *v)]
        written = pl.pallas_call(
            write_kernel,
            out_shape=outs,
            in_specs=[vmem] * 9,
            out_specs=[hbm] * 9,
            scratch_shapes=[dma((16,))],
            compiler_params=pltpu.CompilerParams(vmem_limit_bytes=2**20),
            name="write",
        )(*results)
        new = [r.reshape(t.shape) for r, t in zip(written[:3], weights)]
        moved = [jnp.swapaxes(one, 0, 1) if n % 3 == 2 else one for n, one in enumerate(written[3:])]
        return (*new, *moved)

    all_of, cut = P(None, None, None), P(None, "dp", None)
    return jax.shard_map(
        step,
        mesh=mesh,
        in_specs=(P(("rep", "dp"), None, None, None),) * 3 + (all_of,) * 3 + (cut,) * 6,
        out_specs=(P("rep", None, None),) * 3 + (P("rep", "dp", None),) * 6,
        check_vma=False,
    )
```

time: 1830 us -> 188 us (0.10)
  waiting for transfers between devices: 1630 us -> 0 us
  Pallas kernels: 0 us -> 179 us
  local copies, waits for them, and re-layouts: 107 us -> 8.7 us
  blocking collectives: 69.3 us -> 0 us
    unnamed x9 -> x0, waiting for transfers between devices: 1430 us -> none
    all_gather x3 -> x0, waiting for transfers between devices: 203 us -> none  [step(): whole = [lax.all_gather(one[0], 'dp', axis=1, tiled=True) for one in new]]
    pallas_call x0 -> x2, Pallas kernels: none -> 179 us  [the longest x1 167 us: step(): pl.pallas_call(functools.partial(step_kernel, count), out_shape=blocks +...]
    unnamed x24 -> x4, local copies, waits for them, and re-layouts: 106 us -> 8.7 us
    psum x1 -> x0, blocking collectives: 69.3 us -> none  [step(): squares = lax.psum(sum((jnp.sum(g * g) for g in gradients)), 'dp')]
  transfers between devices with their start and end apart: 6 -> 0, of which waited for: 6 -> 0; matrix products, arithmetic and copies ran while one was open for 4% -> 0% of each run, Pallas kernels for 0% -> 0%
where the time goes in v1:
time: 188 us
  Pallas kernels  179 us (95%)
  local copies, waits for them, and re-layouts  8.7 us (5%)
    pallas_call x1, Pallas kernels, step(): pl.pallas_call(functools.partial(step_kernel, count), out_shape=blocks +...  167 us
    pallas_call x1, Pallas kernels, step(): pl.pallas_call(write_kernel, out_shape=outs, in_specs=[vmem] * 9, out_spe...  11.8 us
    unnamed x4, local copies, waits for them, and re-layouts  8.7 us

profile of v1, /device:TPU:1, one launch (start us, length us, event | category | flops | bytes accessed | tf_op | source)
XLA Modules:
  0.0 188.2 jit_solution(9253702244390305454)
XLA Ops:
  0.6 167.0 %step.1 = (bf16[2,4,4,4,2,8,2816]{6,5,4,3,2,1,0:T(8,128)(2,1)S(1)}, bf16[2,4,4,4,2,8,2816]{6,5,4,3,2,1,0:T(8,128)(2,1)S(1)}, bf16[2,4,4,4,2,11,8,256]{7,6,5,4,3,...) custom-call(bf16[2,4,4,4,2,8,2816]{6,5,4,3,2,1,0:T(8,128)(2,1)} %bit, ...), custom_call_target="tpu_custom_call" | custom-call | tf_op jit(solution)/shard_map/step/pallas_call | solution.py:513
  167.7 0.0 copy-start
  167.7 4.4 %copy-done = bf16[2,4,4,4,2,8,2816]{6,5,4,3,2,1,0:T(8,128)(2,1)} copy-done((bf16[2,4,4,4,2,8,2816]{6,5,4,3,2,1,0:T(8,128)(2,1)}, bf16[2,4,4,4,2,8,2816]{6,5,4,3,2,1,0:T(8,128)(2,1)S(1)}, u32[]{:S(2)}) %copy-start) | copy-done | bytes 11534360
  172.1 0.0 copy-start.1
  172.1 4.3 %copy-done.1 = bf16[2,4,4,4,2,8,2816]{6,5,4,3,2,1,0:T(8,128)(2,1)S(1)} copy-done((bf16[2,4,4,4,2,8,2816]{6,5,4,3,2,1,0:T(8,128)(2,1)S(1)}, bf16[2,4,4,4,2,8,2816]{6,5,4,3,2,1,0:T(8,128)(2,1)}, u32[]{:S(2)}) %copy-start.1) | copy-done | bytes 11534360
  176.4 11.8 %write.1 = (bf16[2,4,4,4,2,8,2816]{6,5,4,3,2,1,0:T(8,128)(2,1)}, bf16[2,4,4,4,2,8,2816]{6,5,4,3,2,1,0:T(8,128)(2,1)}, bf16[2,4,4,2,11,8,1024]{6,5,4,3,2,1,0:T(8,...) custom-call(bf16[2,4,4,4,2,8,2816]{6,5,4,3,2,1,0:T(8,128)(2,1)S(1)} , ...), custom_call_target="tpu_custom_call" | custom-call | tf_op jit(solution)/shard_map/write/pallas_call | solution.py:541
Async XLA Ops:
  167.7 4.4 %copy-start = (bf16[2,4,4,4,2,8,2816]{6,5,4,3,2,1,0:T(8,128)(2,1)}, bf16[2,4,4,4,2,8,2816]{6,5,4,3,2,1,0:T(8,128)(2,1)S(1)}, u32[]{:S(2)}) copy-start(bf16[2,4,4,4,2,8,2816]{6,5,4,3,2,1,0:T(8,128)(2,1)S(1)} %get-tuple-element.27.Wg) | copy-start | bytes 34603012
  172.1 4.3 %copy-start.1 = (bf16[2,4,4,4,2,8,2816]{6,5,4,3,2,1,0:T(8,128)(2,1)S(1)}, bf16[2,4,4,4,2,8,2816]{6,5,4,3,2,1,0:T(8,128)(2,1)}, u32[]{:S(2)}) copy-start(bf16[2,4,4,4,2,8,2816]{6,5,4,3,2,1,0:T(8,128)(2,1)} %copy-done) | copy-start | bytes 34603012

commit v2 on v1

--- a/solution.py
+++ b/solution.py
@@ -86,7 +86,7 @@
         copy(at(i, ALL, a, b, ALL, 1 - k), at(i, ALL, a, b, ALL, 1 - k), d2d_s.at[i, ra, rb], d2d_r.at[i, ra, rb], partner).wait_recv()
 
     across = me - q + (2 - 2 * (q // 2)) + (1 - k)
-    peers = [partner, across] + [near(axis, by) for axis in EACH for by in OTHERS]
+    peers = [partner, across] + [near(axis, by) for axis in EACH for by in AHEAD]
     barrier = pltpu.get_barrier_semaphore()
     for peer in peers:
         pl.semaphore_signal(barrier, inc=1, device_id={"dp": peer}, device_id_type=MESH)
@@ -278,7 +278,7 @@
         if i == 2:
             for n in EACH:
                 copy(quad_g.at[q], quad_g.at[q], x_s.at[n], x_r.at[n], quad[n]).start()
-    norms[0, 0] = squares
+    norms[0, 0] = jnp.sum(squares, axis=0, keepdims=True)
 
     def drain(j):
         for i in EACH:
@@ -293,19 +293,17 @@
             hop_b(i, kind).wait_send()
             hop_c(i, kind).wait_send()
 
-    first = copy(norms.at[0, 0], norms.at[0, 1], n_s.at[0, 1], n_r.at[0, 1], partner)
-    first.start()
-    first.wait()
-    norms[1, 0] = norms[0, 0] + norms[0, 1]
-    for turn, axis in ((1, 2), (2, 1), (3, 0)):
-        hops = [copy(norms.at[turn, 0], norms.at[turn, by], n_s.at[turn, by], n_r.at[turn, by], near(axis, by)) for by in OTHERS]
+    line, plane = lax.rem(me, 8), me // 8
+    for turn, others in ((0, [plane * 8 + lax.rem(line + by, 8) for by in range(1, 8)]), (1, [lax.rem(plane + by, 16) * 8 + line for by in range(1, 16)])):
+        hops = [copy(norms.at[turn, 0], norms.at[turn, by], n_s.at[turn, by], n_r.at[turn, by], to) for by, to in enumerate(others, 1)]
         for hop in hops:
             hop.start()
         for hop in hops:
             hop.wait()
-        norms[turn + 1, 0] = (norms[turn, 0] + norms[turn, 1]) + (norms[turn, 2] + norms[turn, 3])
-    squares = norms[4, 0]
-    squares = jnp.sum(jnp.sum(squares, axis=1, keepdims=True), axis=0, keepdims=True)
+        squares = jnp.sum(norms[turn, 0 : len(hops) + 1], axis=0)
+        if turn == 0:
+            norms[1, 0] = squares
+    squares = jnp.sum(squares, axis=1, keepdims=True)
     factor = jnp.minimum(1.0, 0.5 * lax.rsqrt(squares / count + 1e-30))
 
     def adamw(w, m, v, g):
@@ -399,9 +397,21 @@
         ref = at(i, ALL, rel(i, 0, ra), rel(i, 1, rb), ALL, 1 - k)
         copy(ref, ref, d2d_s.at[i, ra, rb], d2d_r.at[i, ra, rb], partner).wait_recv()
 
-    for i in (0, 1):
+    def spread(i, c):
+        a, b, _ = home[i]
+        ref = at(i, ALL, a, b, c, k)
+        for d in SIDES:
+            copy(ref, ref, b_s.at[i, d], b_r.at[i, d], near(AXES[i][1], AHEAD[d])).start()
+        for d in SIDES:
+            copy(ref, ref, a_s.at[i, d, 0], a_r.at[i, d, 0], near(AXES[i][0], AHEAD[d])).start()
+
+    def begin(i):
         for kind in SIDES:
             back_c(i, kind).start()
+        spread(i, home[i][2])
+
+    begin(0)
+    begin(1)
     for n in EACH:
         copy(piece(n), cols.at[q], x_s.at[3 + n], x_r.at[3 + n], quad[n]).wait_send()
         theirs = cols.at[lax.rem(q + n + 1, 4)]
@@ -410,20 +420,17 @@
         for n in PLACES:
             rows[0, n * n_rows : (n + 1) * n_rows, 0:quarter] = f32(cols[n, l])
         at(2, l, *home[2], k)[...] = rows[0, :, 0:quarter].reshape(n_rows // 2, 8, quarter).astype(BF16)
-    for kind in SIDES:
-        back_c(2, kind).start()
+    begin(2)
     for i in EACH:
         for d in SIDES:
             came_c(i, d)
             back_c(i, 2 + d).start()
+        for d in SIDES:
+            spread(i, rel(i, 2, AHEAD[d]))
     for i in EACH:
         for d in SIDES:
             came_c(i, 2 + d)
-        for kind in SIDES:
-            back_b(i, kind).start()
-    for i in EACH:
-        for kind in SIDES:
-            back_a(i, kind, 0).start()
+        spread(i, rel(i, 2, 2))
         share(i, 0, 0).start()
     for i in EACH:
         for d in SIDES:
@@ -475,17 +482,20 @@
             back_c(i, kind).wait_send()
 
 
-def write_kernel(Wg, Wu, Wd, *refs):
-    small_in, (og, ou, od), outs, sems = refs[:6], refs[6:9], refs[9:15], refs[15]
-    quarter = Wd.shape[-1]
-    copies = [pltpu.make_async_copy(Wg, og, sems.at[14]), pltpu.make_async_copy(Wu, ou, sems.at[15])]
+def write_wide(W, out, *refs):
+    one = pltpu.make_async_copy(W, out, refs[-1].at[0])
+    one.start()
+    one.wait()
+
+
+def write_tall(n_small, W, *refs):
+    small_in, out, small_out, sems = refs[:n_small], refs[n_small], refs[n_small + 1 : -1], refs[-1]
+    quarter = W.shape[-1]
+    copies = [pltpu.make_async_copy(r, o, sems.at[n]) for n, (r, o) in enumerate(zip(small_in, small_out))]
     for n in PLACES:
-        for zh in SIDES:
-            copies.append(
-                pltpu.make_async_copy(Wd.at[:, :, :, 2 * zh + n // 2, n % 2], od.at[:, :, :, zh, :, :, n * quarter : (n + 1) * quarter], sems.at[2 * n + zh])
-            )
-    for n in range(6):
-        copies.append(pltpu.make_async_copy(small_in[n], outs[n], sems.at[8 + n]))
+        for half in SIDES:
+            columns = slice(n * quarter, (n + 1) * quarter)
+            copies.append(pltpu.make_async_copy(W.at[:, :, :, 2 * half + n // 2, n % 2], out.at[:, :, :, half, :, :, columns], sems.at[len(copies)]))
     for one in copies:
         one.start()
     for one in copies:
@@ -529,27 +539,32 @@
                 pltpu.VMEM((2, 4 * n_rows, tall), F32),
                 pltpu.VMEM((LAYERS, n_rows, tall), BF16),
                 pltpu.VMEM((4, LAYERS, n_rows, quarter), BF16),
-                pltpu.VMEM((5, 4, 8, 128), F32),
+                pltpu.VMEM((2, 16, 1, 128), F32),
                 dma((3, 4, 4)), dma((9,)), dma((3, 4, 4)), dma((3, 4, 4)),
                 dma((3, 6, 4)), dma((3, 6, 4)), dma((3, 6)), dma((3, 6)), dma((3, 6)), dma((3, 6)),
-                dma((6,)), dma((6,)), dma((4, 4)), dma((4, 4)),
+                dma((6,)), dma((6,)), dma((2, 16)), dma((2, 16)),
             ],
             compiler_params=pltpu.CompilerParams(collective_id=0, has_side_effects=True, vmem_limit_bytes=26600000),
             name="step",
         )(*g, *w, *m, *v)
-        outs = [jax.ShapeDtypeStruct(s, BF16) for s in shapes] + [jax.ShapeDtypeStruct(one.shape, F32) for one in (*m, *v)]
-        written = pl.pallas_call(
-            write_kernel,
-            out_shape=outs,
-            in_specs=[vmem] * 9,
-            out_specs=[hbm] * 9,
-            scratch_shapes=[dma((16,))],
-            compiler_params=pltpu.CompilerParams(vmem_limit_bytes=2**20),
-            name="write",
-        )(*results)
-        new = [r.reshape(t.shape) for r, t in zip(written[:3], weights)]
-        moved = [jnp.swapaxes(one, 0, 1) if n % 3 == 2 else one for n, one in enumerate(written[3:])]
-        return (*new, *moved)
+
+        def write(kernel, arrays, outs):
+            return pl.pallas_call(
+                kernel,
+                out_shape=outs,
+                in_specs=[vmem] * len(arrays),
+                out_specs=[hbm] * len(outs),
+                scratch_shapes=[dma((16,))],
+                compiler_params=pltpu.CompilerParams(vmem_limit_bytes=2**20),
+                name="write",
+            )(*arrays)
+
+        outs = [jax.ShapeDtypeStruct(s, BF16) for s in shapes]
+        small = results[3:]
+        new_gate, new_up = (write(write_wide, [r], [o])[0] for r, o in zip(results, outs[:2]))
+        new_down, *moved = write(functools.partial(write_tall, len(small)), results[2:], outs[2:] + [jax.ShapeDtypeStruct(one.shape, F32) for one in small])
+        new = [r.reshape(t.shape) for r, t in zip((new_gate, new_up, new_down), weights)]
+        return (*new, *(jnp.swapaxes(one, 0, 1) if n % 3 == 2 else one for n, one in enumerate(moved)))
 
     all_of, cut = P(None, None, None), P(None, "dp", None)
     return jax.shard_map(

time: 188 us -> 175 us (0.931)
  local copies, waits for them, and re-layouts: 8.7 us -> 0 us
  Pallas kernels: 179 us -> 174 us
    unnamed x4 -> x0, local copies, waits for them, and re-layouts: 8.7 us -> none
    pallas_call x1, Pallas kernels: 167 us -> 160 us  [step(): pl.pallas_call(functools.partial(step_kernel, count), out_shape=blocks +...]
    pallas_call x1 -> x3, Pallas kernels: 11.8 us -> 13.9 us  [write(): pl.pallas_call(kernel, out_shape=outs, in_specs=[vmem] * len(arrays), out...]
where the time goes in v2:
time: 175 us
  Pallas kernels  174 us (99%)
    pallas_call x1, Pallas kernels, step(): pl.pallas_call(functools.partial(step_kernel, count), out_shape=blocks +...  160 us
    pallas_call x3, Pallas kernels, write(): pl.pallas_call(kernel, out_shape=outs, in_specs=[vmem] * len(arrays), out...  13.9 us

profile of v2, /device:TPU:1, one launch (start us, length us, event | category | flops | bytes accessed | tf_op | source)
XLA Modules:
  0.0 174.7 jit_solution(1495834386469781918)
XLA Ops:
  0.6 160.1 %step.1 = (bf16[2,4,4,4,2,8,2816]{6,5,4,3,2,1,0:T(8,128)(2,1)S(1)}, bf16[2,4,4,4,2,8,2816]{6,5,4,3,2,1,0:T(8,128)(2,1)S(1)}, bf16[2,4,4,4,2,11,8,256]{7,6,5,4,3,...) custom-call(bf16[2,4,4,4,2,8,2816]{6,5,4,3,2,1,0:T(8,128)(2,1)} %bit, ...), custom_call_target="tpu_custom_call" | custom-call | tf_op jit(solution)/shard_map/step/pallas_call | solution.py:523
  160.8 4.6 %write.3 = bf16[2,4,4,4,2,8,2816]{6,5,4,3,2,1,0:T(8,128)(2,1)} custom-call(bf16[2,4,4,4,2,8,2816]{6,5,4,3,2,1,0:T(8,128)(2,1)S(1)} %get-tuple-element.25.W), custom_call_target="tpu_custom_call" | custom-call | tf_op jit(solution)/shard_map/write/pallas_call | solution.py:552
  165.3 4.6 %write.4 = bf16[2,4,4,4,2,8,2816]{6,5,4,3,2,1,0:T(8,128)(2,1)} custom-call(bf16[2,4,4,4,2,8,2816]{6,5,4,3,2,1,0:T(8,128)(2,1)S(1)} %get-tuple-element.26.W), custom_call_target="tpu_custom_call" | custom-call | tf_op jit(solution)/shard_map/write/pallas_call | solution.py:552
  169.9 4.8 %write.5 = (bf16[2,4,4,2,11,8,1024]{6,5,4,3,2,1,0:T(8,128)(2,1)}, f32[2,8,2816]{2,1,0:T(8,128)}, f32[2,8,2816]{2,1,0:T(8,128)}, f32[22,2,1024]{2,1,0:T(2,128)}, ...) custom-call(bf16[2,4,4,4,2,11,8,256]{7,6,5,4,3,2,1,0:T(8,128)(2,1)S(1)} %get-tuple-element.27.W, ...), custom_call_target="tpu_custom_call" | custom-call | tf_op jit(solution)/shard_map/write/pallas_call | solution.py:552

commit v3 on v2

--- a/solution.py
+++ b/solution.py
@@ -11,6 +11,8 @@
 F32, BF16 = jnp.float32, jnp.bfloat16
 AXES = ((0, 1, 2), (1, 2, 0), (2, 0, 1))
 LAYERS = 2
+A, B, C = range(3)
+FAR = 2
 EACH, SIDES, PLACES, OTHERS, LANDED = range(3), range(2), range(4), range(1, 4), range(2, 6)
 AHEAD, BEHIND = (1, 3), (3, 1)
 
@@ -19,8 +21,8 @@
     return lax.rem(2 + j + (j // 2) * (2 * j - 3), 4)
 
 
-def loop(body, n=4):
-    lax.fori_loop(0, n, lambda j, c: (body(j), c)[1], 0)
+def loop(body, n=4, start=0):
+    lax.fori_loop(start, n, lambda j, c: (body(j), c)[1], 0)
 
 
 def f32(x):
@@ -32,7 +34,7 @@
     Wg, Wu, Wd, mg2, mu2, md2, vg2, vu2, vd2,
     R1g, R1u, R1d, R2g, R2u, R2d, Q1g, Q1u, Q1d, Q2g, Q2u, Q2d, P1g, P1u, P1d, P2g, P2u, P2d,
     own_g, own_u, own_d, quad_g, rows, new_rows, cols, norms,
-    load_sem, own_sem, d2d_s, d2d_r, a_s, a_r, b_s, b_r, c_s, c_r, x_s, x_r, n_s, n_r,
+    load_sem, own_sem, d2d_s, d2d_r, a_s, a_r, b_s, b_r, c_s, c_r, x_s, x_r, n_s, n_r, piece_l, piece_r, tail_r,
 ):
     g_in, W, w_in = (gg, gu, gd), (Wg, Wu, Wd), (wg, wu, wd)
     R1, R2, Q1, Q2, P1, P2 = (R1g, R1u, R1d), (R2g, R2u, R2d), (Q1g, Q1u, Q1d), (Q2g, Q2u, Q2d), (P1g, P1u, P1d), (P2g, P2u, P2d)
@@ -64,24 +66,38 @@
     def rel(i, which, by):
         return lax.rem(home[i][which] + by, 4)
 
-    def source(i, a, b, core):
+    def source(i, a, b, c, core):
         if i == 0:
-            return gg.at[:, a, b, :, core]
+            return gg.at[:, a, b, c, core]
         if i == 1:
-            return gu.at[:, :, a, b, core]
+            return gu.at[:, c, a, b, core]
         columns = pl.ds(pl.multiple_of(lax.rem(a, 2) * (2 * quarter) + core * quarter, quarter), quarter)
-        return gd.at[:, b, :, a // 2, :, :, columns]
+        return gd.at[:, b, c, a // 2, :, :, columns]
 
     def load(i, ra, rb):
-        a, b = rel(i, 0, ra), rel(i, 1, rb)
-        return pltpu.make_async_copy(source(i, a, b, k), at(i, ALL, a, b, ALL, k), load_sem.at[i, ra, rb])
+        a, b = rel(i, A, ra), rel(i, B, rb)
+        return pltpu.make_async_copy(source(i, a, b, ALL, k), at(i, ALL, a, b, ALL, k), load_sem.at[i, ra, rb])
 
     def trade(i, ra, rb):
-        a, b = rel(i, 0, ra), rel(i, 1, rb)
-        return copy(source(i, a, b, 1 - k), at(i, ALL, a, b, ALL, k), d2d_s.at[i, ra, rb], d2d_r.at[i, ra, rb], partner)
+        a, b = rel(i, A, ra), rel(i, B, rb)
+        return copy(source(i, a, b, ALL, 1 - k), at(i, ALL, a, b, ALL, k), d2d_s.at[i, ra, rb], d2d_r.at[i, ra, rb], partner)
+
+    def first_load(i, c):
+        a, b = rel(i, A, FAR), rel(i, B, FAR)
+        return pltpu.make_async_copy(source(i, a, b, c, k), at(i, ALL, a, b, c, k), piece_l.at[i, c])
+
+    def first_trade(i, c):
+        a, b = rel(i, A, FAR), rel(i, B, FAR)
+        return copy(source(i, a, b, c, 1 - k), at(i, ALL, a, b, c, k), d2d_s.at[i, 2, 2], piece_r.at[i, c], partner)
+
+    def first_traded(i, c):
+        a, b = rel(i, A, FAR), rel(i, B, FAR)
+        first_load(i, c).wait()
+        ref = at(i, ALL, a, b, c, 1 - k)
+        copy(ref, ref, d2d_s.at[i, 2, 2], piece_r.at[i, c], partner).wait_recv()
 
     def traded(i, ra, rb):
-        a, b = rel(i, 0, ra), rel(i, 1, rb)
+        a, b = rel(i, A, ra), rel(i, B, rb)
         load(i, ra, rb).wait()
         copy(at(i, ALL, a, b, ALL, 1 - k), at(i, ALL, a, b, ALL, 1 - k), d2d_s.at[i, ra, rb], d2d_r.at[i, ra, rb], partner).wait_recv()
 
@@ -91,21 +107,29 @@
     for peer in peers:
         pl.semaphore_signal(barrier, inc=1, device_id={"dp": peer}, device_id_type=MESH)
 
-    for ras in ((2,), (1, 3), (0,)):
-        def start_loads(j, ras=ras):
+    def start_all(what, ras, start=0):
+        def body(j):
             for ra in ras:
                 for i in EACH:
-                    load(i, ra, order(j)).start()
-        if ras == (2,):
-            loop(start_loads)
-            pl.semaphore_wait(barrier, len(peers))
-        else:
-            loop(start_loads)
-        def start_trades(j, ras=ras):
-            for ra in ras:
-                for i in EACH:
-                    trade(i, ra, order(j)).start()
-        loop(start_trades)
+                    what(i, ra, order(j)).start()
+
+        loop(body, start=start)
+
+    def start_first(what):
+        def body(c):
+            for i in EACH:
+                what(i, c).start()
+
+        loop(body)
+
+    start_first(first_load)
+    start_all(load, (2,), 1)
+    pl.semaphore_wait(barrier, len(peers))
+    start_first(first_trade)
+    start_all(trade, (2,), 1)
+    for ras in (AHEAD, (0,)):
+        start_all(load, ras)
+        start_all(trade, ras)
     own = [
         pltpu.make_async_copy(wg.at[:, pos[0], pos[1], pos[2], k], own_g, own_sem.at[0]),
         pltpu.make_async_copy(wu.at[:, pos[0], pos[1], pos[2], k], own_u, own_sem.at[1]),
@@ -129,34 +153,34 @@
         return sum2(i, l, home[i][2]) + f32(P2[i][0, l]) + f32(P2[i][1, l])
 
     def hop_a(i, kind, rb):
-        d, b = kind % 2, rel(i, 1, rb)
+        d, b = kind % 2, rel(i, B, rb)
         to = near(AXES[i][0], AHEAD[d])
         if kind < 2:
-            src, dst = at(i, d, rel(i, 0, 2), b, ALL, k), R1[i].at[d, b]
+            src, dst = at(i, d, rel(i, A, FAR), b, ALL, k), R1[i].at[d, b]
         elif kind < 4:
-            src, dst = at(i, 1 - d, rel(i, 0, AHEAD[d]), b, ALL, k), R2[i].at[d, 1 - d, b]
+            src, dst = at(i, 1 - d, rel(i, A, AHEAD[d]), b, ALL, k), R2[i].at[d, 1 - d, b]
         else:
             src, dst = R1[i].at[d, b], R2[i].at[d, d, b]
         return copy(src, dst, a_s.at[i, kind, rb], a_r.at[i, kind, rb], to)
 
-    def hop_b(i, kind):
-        d = kind % 2
+    def hop_b(i, kind, rc):
+        d, c = kind % 2, rel(i, C, rc)
         to = near(AXES[i][1], AHEAD[d])
         if kind < 2:
-            src, dst = R2[i].at[0, d, rel(i, 1, 2)], Q1[i].at[d]
+            src, dst = R2[i].at[0, d, rel(i, B, FAR), c], Q1[i].at[d, c]
         elif kind < 4:
-            src, dst = R2[i].at[0, 1 - d, rel(i, 1, AHEAD[d])], Q2[i].at[d, 1 - d]
+            src, dst = R2[i].at[0, 1 - d, rel(i, B, AHEAD[d]), c], Q2[i].at[d, 1 - d, c]
         else:
-            src, dst = Q1[i].at[d], Q2[i].at[d, d]
-        return copy(src, dst, b_s.at[i, kind], b_r.at[i, kind], to)
+            src, dst = Q1[i].at[d, c], Q2[i].at[d, d, c]
+        return copy(src, dst, b_s.at[i, kind, rc], b_r.at[i, kind, rc], to)
 
     def hop_c(i, kind):
         d = kind % 2
         to = near(AXES[i][2], AHEAD[d])
         if kind < 2:
-            src, dst = Q2[i].at[0, d, rel(i, 2, 2)], P1[i].at[d]
+            src, dst = Q2[i].at[0, d, rel(i, C, FAR)], P1[i].at[d]
         elif kind < 4:
-            src, dst = Q2[i].at[0, 1 - d, rel(i, 2, AHEAD[d])], P2[i].at[d, 1 - d]
+            src, dst = Q2[i].at[0, 1 - d, rel(i, C, AHEAD[d])], P2[i].at[d, 1 - d]
         else:
             src, dst = P1[i].at[d], P2[i].at[d, d]
         return copy(src, dst, c_s.at[i, kind], c_r.at[i, kind], to)
@@ -165,7 +189,7 @@
         rb = order(j)
         for i in EACH:
             traded(i, 2, rb)
-            a, b = rel(i, 0, 2), rel(i, 1, rb)
+            a, b = rel(i, A, FAR), rel(i, B, rb)
 
             def add(t):
                 at(i, t // 4, a, b, lax.rem(t, 4), k)[...] = sum0(i, t // 4, a, b, lax.rem(t, 4)).astype(BF16)
@@ -174,7 +198,17 @@
             hop_a(i, 0, rb).start()
             hop_a(i, 1, rb).start()
 
-    loop(farthest)
+    def farthest_first(c):
+        for i in EACH:
+            first_traded(i, c)
+            a, b = rel(i, A, FAR), rel(i, B, FAR)
+            for l in SIDES:
+                ref = at(i, l, a, b, c, k)
+                ref[...] = sum0(i, l, a, b, c).astype(BF16)
+                copy(ref, R1[i].at[l, b, c], a_s.at[i, l, 2], a_r.at[i, l, 2], near(AXES[i][0], AHEAD[l])).start()
+
+    loop(farthest_first)
+    loop(farthest, start=1)
 
     def plain(j):
         rb = order(j)
@@ -182,7 +216,7 @@
             for d in SIDES:
                 ra = AHEAD[d]
                 traded(i, ra, rb)
-                a, b = rel(i, 0, ra), rel(i, 1, rb)
+                a, b = rel(i, A, ra), rel(i, B, rb)
 
                 def add(c):
                     at(i, 1 - d, a, b, c, k)[...] = sum0(i, 1 - d, a, b, c).astype(BF16)
@@ -197,7 +231,7 @@
         for i in EACH:
             for d in SIDES:
                 hop_a(i, d, rb).wait_recv()
-                a, b = rel(i, 0, AHEAD[d]), rel(i, 1, rb)
+                a, b = rel(i, A, AHEAD[d]), rel(i, B, rb)
 
                 def add(c):
                     R1[i][d, b, c] = (f32(R1[i][d, b, c]) + sum0(i, d, a, b, c)).astype(BF16)
@@ -212,53 +246,63 @@
         for kind in LANDED:
             hop_a(i, kind, rb).wait_recv()
 
-    def settle_a(i, l, rb):
-        b = rel(i, 1, rb)
-
-        def add(c):
-            R2[i][0, l, b, c] = sum1(i, l, b, c).astype(BF16)
-
-        loop(add)
+    def settle_a(i, l, rb, rc):
+        b, c = rel(i, B, rb), rel(i, C, rc)
+        R2[i][0, l, b, c] = sum1(i, l, b, c).astype(BF16)
 
     for i in EACH:
         arrived_a(i, 2)
-        for d in SIDES:
-            settle_a(i, d, 2)
-            hop_b(i, d).start()
-    for rb, d in ((3, 1), (1, 0)):
+
+        def far_b(j, i=i):
+            for d in SIDES:
+                settle_a(i, d, 2, order(j))
+                hop_b(i, d, order(j)).start()
+
+        loop(far_b)
+    for rb in AHEAD:
         for i in EACH:
             arrived_a(i, rb)
-            settle_a(i, 1 - d, rb)
-            hop_b(i, 2 + d).start()
-    for i in EACH:
-        for d in SIDES:
-            hop_b(i, d).wait_recv()
-            b = rel(i, 1, AHEAD[d])
-
-            def add(c, i=i, d=d, b=b):
-                Q1[i][d, c] = (f32(Q1[i][d, c]) + sum1(i, d, b, c)).astype(BF16)
-
-            loop(add)
-            hop_b(i, 4 + d).start()
-
+
+    def near_b(j):
+        rc = order(j)
+        for i in EACH:
+            for d in SIDES:
+                settle_a(i, 1 - d, AHEAD[d], rc)
+                hop_b(i, 2 + d, rc).start()
+        for i in EACH:
+            for d in SIDES:
+                hop_b(i, d, rc).wait_recv()
+                c = rel(i, C, rc)
+                Q1[i][d, c] = (f32(Q1[i][d, c]) + sum1(i, d, rel(i, B, AHEAD[d]), c)).astype(BF16)
+                hop_b(i, 4 + d, rc).start()
+
+    loop(near_b)
     for i in EACH:
         arrived_a(i, 0)
-    for i in EACH:
+
+    def arrived_b(i, rc):
         for kind in LANDED:
-            hop_b(i, kind).wait_recv()
-        for d in SIDES:
-            c = rel(i, 2, 2)
+            hop_b(i, kind, rc).wait_recv()
+
+    for i in EACH:
+        arrived_b(i, 2)
+        for d in SIDES:
+            c = rel(i, C, FAR)
             Q2[i][0, d, c] = sum2(i, d, c).astype(BF16)
             hop_c(i, d).start()
-        for d in SIDES:
-            c = rel(i, 2, AHEAD[d])
+    for d in (1, 0):
+        for i in EACH:
+            arrived_b(i, AHEAD[d])
+            c = rel(i, C, AHEAD[d])
             Q2[i][0, 1 - d, c] = sum2(i, 1 - d, c).astype(BF16)
             hop_c(i, 2 + d).start()
     for i in EACH:
         for d in SIDES:
             hop_c(i, d).wait_recv()
-            P1[i][d] = (f32(P1[i][d]) + sum2(i, d, rel(i, 2, AHEAD[d]))).astype(BF16)
+            P1[i][d] = (f32(P1[i][d]) + sum2(i, d, rel(i, C, AHEAD[d]))).astype(BF16)
             hop_c(i, 4 + d).start()
+    for i in EACH:
+        arrived_b(i, 0)
     squares = jnp.zeros((8, 128), F32)
     for i in (2, 0, 1):
         for kind in LANDED:
@@ -284,13 +328,13 @@
         for i in EACH:
             for kind in range(6):
                 hop_a(i, kind, j).wait_send()
+                hop_b(i, kind, j).wait_send()
             for ra in PLACES:
                 trade(i, ra, j).wait_send()
 
     loop(drain)
     for i in EACH:
         for kind in range(6):
-            hop_b(i, kind).wait_send()
             hop_c(i, kind).wait_send()
 
     line, plane = lax.rem(me, 8), me // 8
@@ -353,13 +397,13 @@
         if kind < 2:
             ref = at(i, ALL, a, b, c, k)
         else:
-            ref = at(i, d, a, b, rel(i, 2, BEHIND[d]), k)
+            ref = at(i, d, a, b, rel(i, C, BEHIND[d]), k)
         return copy(ref, ref, c_s.at[i, kind], c_r.at[i, kind], near(AXES[i][2], AHEAD[d]))
 
     def came_c(i, kind):
         d = kind % 2
         a, b, _ = home[i]
-        ref = at(i, ALL, a, b, rel(i, 2, BEHIND[d]), k) if kind < 2 else at(i, d, a, b, rel(i, 2, 2), k)
+        ref = at(i, ALL, a, b, rel(i, C, BEHIND[d]), k) if kind < 2 else at(i, d, a, b, rel(i, C, FAR), k)
         copy(ref, ref, c_s.at[i, kind], c_r.at[i, kind], partner).wait_recv()
 
     def back_b(i, kind):
@@ -368,40 +412,40 @@
         if kind < 2:
             ref = at(i, ALL, a, b, ALL, k)
         else:
-            ref = at(i, d, a, rel(i, 1, BEHIND[d]), ALL, k)
-        return copy(ref, ref, b_s.at[i, kind], b_r.at[i, kind], near(AXES[i][1], AHEAD[d]))
+            ref = at(i, d, a, rel(i, B, BEHIND[d]), ALL, k)
+        return copy(ref, ref, b_s.at[i, kind, 0], b_r.at[i, kind, 0], near(AXES[i][1], AHEAD[d]))
 
     def came_b(i, kind):
         d = kind % 2
-        ref = at(i, ALL, home[i][0], rel(i, 1, BEHIND[d]), ALL, k) if kind < 2 else at(i, d, home[i][0], rel(i, 1, 2), ALL, k)
-        copy(ref, ref, b_s.at[i, kind], b_r.at[i, kind], partner).wait_recv()
+        ref = at(i, ALL, home[i][0], rel(i, B, BEHIND[d]), ALL, k) if kind < 2 else at(i, d, home[i][0], rel(i, B, FAR), ALL, k)
+        copy(ref, ref, b_s.at[i, kind, 0], b_r.at[i, kind, 0], partner).wait_recv()
 
     def back_a(i, kind, rb):
-        d, b = kind % 2, rel(i, 1, rb)
+        d, b = kind % 2, rel(i, B, rb)
         if kind < 2:
             ref = at(i, ALL, home[i][0], b, ALL, k)
         else:
-            ref = at(i, d, rel(i, 0, BEHIND[d]), b, ALL, k)
+            ref = at(i, d, rel(i, A, BEHIND[d]), b, ALL, k)
         return copy(ref, ref, a_s.at[i, kind, rb], a_r.at[i, kind, rb], near(AXES[i][0], AHEAD[d]))
 
     def came_a(i, kind, rb):
-        d, b = kind % 2, rel(i, 1, rb)
-        ref = at(i, ALL, rel(i, 0, BEHIND[d]), b, ALL, k) if kind < 2 else at(i, d, rel(i, 0, 2), b, ALL, k)
+        d, b = kind % 2, rel(i, B, rb)
+        ref = at(i, ALL, rel(i, A, BEHIND[d]), b, ALL, k) if kind < 2 else at(i, d, rel(i, A, FAR), b, ALL, k)
         copy(ref, ref, a_s.at[i, kind, rb], a_r.at[i, kind, rb], partner).wait_recv()
 
     def share(i, ra, rb):
-        ref = at(i, ALL, rel(i, 0, ra), rel(i, 1, rb), ALL, k)
+        ref = at(i, ALL, rel(i, A, ra), rel(i, B, rb), ALL, k)
         return copy(ref, ref, d2d_s.at[i, ra, rb], d2d_r.at[i, ra, rb], partner)
 
     def shared(i, ra, rb):
-        ref = at(i, ALL, rel(i, 0, ra), rel(i, 1, rb), ALL, 1 - k)
+        ref = at(i, ALL, rel(i, A, ra), rel(i, B, rb), ALL, 1 - k)
         copy(ref, ref, d2d_s.at[i, ra, rb], d2d_r.at[i, ra, rb], partner).wait_recv()
 
     def spread(i, c):
         a, b, _ = home[i]
         ref = at(i, ALL, a, b, c, k)
         for d in SIDES:
-            copy(ref, ref, b_s.at[i, d], b_r.at[i, d], near(AXES[i][1], AHEAD[d])).start()
+            copy(ref, ref, b_s.at[i, d, 0], b_r.at[i, d, 0], near(AXES[i][1], AHEAD[d])).start()
         for d in SIDES:
             copy(ref, ref, a_s.at[i, d, 0], a_r.at[i, d, 0], near(AXES[i][0], AHEAD[d])).start()
 
@@ -426,11 +470,11 @@
             came_c(i, d)
             back_c(i, 2 + d).start()
         for d in SIDES:
-            spread(i, rel(i, 2, AHEAD[d]))
+            spread(i, rel(i, C, AHEAD[d]))
     for i in EACH:
         for d in SIDES:
             came_c(i, 2 + d)
-        spread(i, rel(i, 2, 2))
+        spread(i, rel(i, C, FAR))
         share(i, 0, 0).start()
     for i in EACH:
         for d in SIDES:
@@ -456,7 +500,25 @@
                 back_a(i, 2 + d, rb).start()
                 share(i, BEHIND[d], rb).start()
 
-    loop(pass_on)
+    loop(pass_on, 3)
+
+    def tail(i, d, c):
+        ref = at(i, d, rel(i, A, BEHIND[d]), rel(i, B, FAR), c, k)
+        return copy(ref, ref, a_s.at[i, 2 + d, 2], tail_r.at[i, d, c], near(AXES[i][0], AHEAD[d]))
+
+    for i in EACH:
+        for d in SIDES:
+            came_a(i, d, 2)
+
+    def pass_tail(c):
+        for i in EACH:
+            for d in SIDES:
+                tail(i, d, c).start()
+
+    loop(pass_tail)
+    for i in EACH:
+        for d in SIDES:
+            share(i, BEHIND[d], 2).start()
 
     def last(j):
         rb = lax.rem(order(j) + 2, 4)
@@ -465,7 +527,17 @@
                 came_a(i, 2 + d, rb)
             share(i, 2, rb).start()
 
-    loop(last)
+    loop(last, 3)
+
+    def last_tail(c):
+        for i in EACH:
+            for d in SIDES:
+                ref = at(i, d, rel(i, A, FAR), rel(i, B, FAR), c, k)
+                copy(ref, ref, a_s.at[i, 2 + d, 2], tail_r.at[i, d, c], partner).wait_recv()
+            ref = at(i, ALL, rel(i, A, FAR), rel(i, B, FAR), c, k)
+            copy(ref, ref, d2d_s.at[i, 2, 2], d2d_r.at[i, 2, 2], partner).start()
+
+    loop(last_tail)
 
     def finish(j):
         for i in EACH:
@@ -482,10 +554,15 @@
             back_c(i, kind).wait_send()
 
 
-def write_wide(W, out, *refs):
-    one = pltpu.make_async_copy(W, out, refs[-1].at[0])
-    one.start()
-    one.wait()
+def write_wide(n_wide, *refs):
+    sems = refs[-1]
+    copies = [
+        pltpu.make_async_copy(W.at[l, n], out.at[l, n], sems.at[8 * i + 4 * l + n]) for i, (W, out) in enumerate(zip(refs[:n_wide], refs[n_wide:-1])) for l in SIDES for n in PLACES
+    ]
+    for one in copies:
+        one.start()
+    for one in copies:
+        one.wait()
 
 
 def write_tall(n_small, W, *refs):
@@ -541,8 +618,8 @@
                 pltpu.VMEM((4, LAYERS, n_rows, quarter), BF16),
                 pltpu.VMEM((2, 16, 1, 128), F32),
                 dma((3, 4, 4)), dma((9,)), dma((3, 4, 4)), dma((3, 4, 4)),
-                dma((3, 6, 4)), dma((3, 6, 4)), dma((3, 6)), dma((3, 6)), dma((3, 6)), dma((3, 6)),
-                dma((6,)), dma((6,)), dma((2, 16)), dma((2, 16)),
+                dma((3, 6, 4)), dma((3, 6, 4)), dma((3, 6, 4)), dma((3, 6, 4)), dma((3, 6)), dma((3, 6)),
+                dma((6,)), dma((6,)), dma((2, 16)), dma((2, 16)), dma((3, 4)), dma((3, 4)), dma((3, 2, 4)),
             ],
             compiler_params=pltpu.CompilerParams(collective_id=0, has_side_effects=True, vmem_limit_bytes=26600000),
             name="step",
@@ -561,7 +638,7 @@
 
         outs = [jax.ShapeDtypeStruct(s, BF16) for s in shapes]
         small = results[3:]
-        new_gate, new_up = (write(write_wide, [r], [o])[0] for r, o in zip(results, outs[:2]))
+        new_gate, new_up = write(functools.partial(write_wide, 2), results[:2], outs[:2])
         new_down, *moved = write(functools.partial(write_tall, len(small)), results[2:], outs[2:] + [jax.ShapeDtypeStruct(one.shape, F32) for one in small])
         new = [r.reshape(t.shape) for r, t in zip((new_gate, new_up, new_down), weights)]
         return (*new, *(jnp.swapaxes(one, 0, 1) if n % 3 == 2 else one for n, one in enumerate(moved)))

time: 175 us -> 170 us (0.971)
  Pallas kernels: 174 us -> 169 us
    pallas_call x1, Pallas kernels: 160 us -> 157 us  [step(): pl.pallas_call(functools.partial(step_kernel, count), out_shape=blocks +...]
    pallas_call x3 -> x2, Pallas kernels: 13.9 us -> 12.6 us  [write(): pl.pallas_call(kernel, out_shape=outs, in_specs=[vmem] * len(arrays), out...]
where the time goes in v3:
time: 170 us
  Pallas kernels  169 us (99%)
    pallas_call x1, Pallas kernels, step(): pl.pallas_call(functools.partial(step_kernel, count), out_shape=blocks +...  157 us
    pallas_call x2, Pallas kernels, write(): pl.pallas_call(kernel, out_shape=outs, in_specs=[vmem] * len(arrays), out...  12.6 us

profile of v3, /device:TPU:1, one launch (start us, length us, event | category | flops | bytes accessed | tf_op | source)
XLA Modules:
  0.0 170.1 jit_solution(9962720669128580994)
XLA Ops:
  0.6 156.8 %step.1 = (bf16[2,4,4,4,2,8,2816]{6,5,4,3,2,1,0:T(8,128)(2,1)S(1)}, bf16[2,4,4,4,2,8,2816]{6,5,4,3,2,1,0:T(8,128)(2,1)S(1)}, bf16[2,4,4,4,2,11,8,256]{7,6,5,4,3,...) custom-call(bf16[2,4,4,4,2,8,2816]{6,5,4,3,2,1,0:T(8,128)(2,1)} %bit, ...), custom_call_target="tpu_custom_call" | custom-call | tf_op jit(solution)/shard_map/step/pallas_call | solution.py:600
  157.4 7.9 %write.2 = (bf16[2,4,4,4,2,8,2816]{6,5,4,3,2,1,0:T(8,128)(2,1)}, bf16[2,4,4,4,2,8,2816]{6,5,4,3,2,1,0:T(8,128)(2,1)}) custom-call(bf16[2,4,4,4,2,8,2816]{6,5,4,3,2,1,0:T(8,128)(2,1)S(1)} %get-tuple-element.27.refs_0_, bf16[2,4,4,4,2,8,2816]{6,5,4,3,2,1,0:T(8,128)(2,1)S(1)} %get-tuple-element.28.refs_1_), custom_call_target="tpu_custom_call" | custom-call | tf_op jit(solution)/shard_map/write/pallas_call | solution.py:629
  165.3 4.8 %write.3 = (bf16[2,4,4,2,11,8,1024]{6,5,4,3,2,1,0:T(8,128)(2,1)}, f32[2,8,2816]{2,1,0:T(8,128)}, f32[2,8,2816]{2,1,0:T(8,128)}, f32[22,2,1024]{2,1,0:T(2,128)}, ...) custom-call(bf16[2,4,4,4,2,11,8,256]{7,6,5,4,3,2,1,0:T(8,128)(2,1)S(1)} %get-tuple-element.31.W, ...), custom_call_target="tpu_custom_call" | custom-call | tf_op jit(solution)/shard_map/write/pallas_call | solution.py:629

commit v4 on v3

--- a/solution.py
+++ b/solution.py
@@ -18,7 +18,7 @@
 
 
 def order(j):
-    return lax.rem(2 + j + (j // 2) * (2 * j - 3), 4)
+    return lax.rem(2 + j + lax.div(j, 2) * (2 * j - 3), 4)
 
 
 def loop(body, n=4, start=0):
@@ -34,7 +34,7 @@
     Wg, Wu, Wd, mg2, mu2, md2, vg2, vu2, vd2,
     R1g, R1u, R1d, R2g, R2u, R2d, Q1g, Q1u, Q1d, Q2g, Q2u, Q2d, P1g, P1u, P1d, P2g, P2u, P2d,
     own_g, own_u, own_d, quad_g, rows, new_rows, cols, norms,
-    load_sem, own_sem, d2d_s, d2d_r, a_s, a_r, b_s, b_r, c_s, c_r, x_s, x_r, n_s, n_r, piece_l, piece_r, tail_r,
+    load_sem, own_sem, d2d_s, d2d_r, a_s, a_r, b_s, b_r, c_s, c_r, x_s, x_r, n_s, n_r, piece_l, piece_r, tail_r, share_r,
 ):
     g_in, W, w_in = (gg, gu, gd), (Wg, Wu, Wd), (wg, wu, wd)
     R1, R2, Q1, Q2, P1, P2 = (R1g, R1u, R1d), (R2g, R2u, R2d), (Q1g, Q1u, Q1d), (Q2g, Q2u, Q2d), (P1g, P1u, P1d), (P2g, P2u, P2d)
@@ -63,8 +63,18 @@
     ALL = slice(None)
     home = [[pos[n] for n in AXES[i]] for i in EACH]
 
+    around = [[lax.rem(one + by, 4) for by in PLACES] for one in pos]
+
     def rel(i, which, by):
+        if isinstance(by, int):
+            return around[AXES[i][which]][by]
         return lax.rem(home[i][which] + by, 4)
+
+    def sent(ref, sem):
+        copy(ref, ref, sem, x_r.at[0], partner).wait_send()
+
+    def landed(ref, sem):
+        copy(ref, ref, x_s.at[0], sem, partner).wait_recv()
 
     def source(i, a, b, c, core):
         if i == 0:
@@ -80,7 +90,7 @@
 
     def trade(i, ra, rb):
         a, b = rel(i, A, ra), rel(i, B, rb)
-        return copy(source(i, a, b, ALL, 1 - k), at(i, ALL, a, b, ALL, k), d2d_s.at[i, ra, rb], d2d_r.at[i, ra, rb], partner)
+        return copy(source(i, a, b, ALL, 1 - k), at(i, ALL, a, b, ALL, k), d2d_s.at[i], d2d_r.at[i, ra, rb], partner)
 
     def first_load(i, c):
         a, b = rel(i, A, FAR), rel(i, B, FAR)
@@ -88,18 +98,18 @@
 
     def first_trade(i, c):
         a, b = rel(i, A, FAR), rel(i, B, FAR)
-        return copy(source(i, a, b, c, 1 - k), at(i, ALL, a, b, c, k), d2d_s.at[i, 2, 2], piece_r.at[i, c], partner)
+        return copy(source(i, a, b, c, 1 - k), at(i, ALL, a, b, c, k), d2d_s.at[i], piece_r.at[i, c], partner)
 
     def first_traded(i, c):
         a, b = rel(i, A, FAR), rel(i, B, FAR)
         first_load(i, c).wait()
         ref = at(i, ALL, a, b, c, 1 - k)
-        copy(ref, ref, d2d_s.at[i, 2, 2], piece_r.at[i, c], partner).wait_recv()
+        copy(ref, ref, d2d_s.at[i], piece_r.at[i, c], partner).wait_recv()
 
     def traded(i, ra, rb):
         a, b = rel(i, A, ra), rel(i, B, rb)
         load(i, ra, rb).wait()
-        copy(at(i, ALL, a, b, ALL, 1 - k), at(i, ALL, a, b, ALL, 1 - k), d2d_s.at[i, ra, rb], d2d_r.at[i, ra, rb], partner).wait_recv()
+        copy(at(i, ALL, a, b, ALL, 1 - k), at(i, ALL, a, b, ALL, 1 - k), d2d_s.at[i], d2d_r.at[i, ra, rb], partner).wait_recv()
 
     across = me - q + (2 - 2 * (q // 2)) + (1 - k)
     peers = [partner, across] + [near(axis, by) for axis in EACH for by in AHEAD]
@@ -161,7 +171,7 @@
             src, dst = at(i, 1 - d, rel(i, A, AHEAD[d]), b, ALL, k), R2[i].at[d, 1 - d, b]
         else:
             src, dst = R1[i].at[d, b], R2[i].at[d, d, b]
-        return copy(src, dst, a_s.at[i, kind, rb], a_r.at[i, kind, rb], to)
+        return copy(src, dst, a_s.at[i, min(kind // 2, 1)], a_r.at[i, min(kind, 2), rb], to)
 
     def hop_b(i, kind, rc):
         d, c = kind % 2, rel(i, C, rc)
@@ -172,7 +182,7 @@
             src, dst = R2[i].at[0, 1 - d, rel(i, B, AHEAD[d]), c], Q2[i].at[d, 1 - d, c]
         else:
             src, dst = Q1[i].at[d, c], Q2[i].at[d, d, c]
-        return copy(src, dst, b_s.at[i, kind, rc], b_r.at[i, kind, rc], to)
+        return copy(src, dst, b_s.at[i, min(kind // 2, 1)], b_r.at[i, min(kind, 2), rc], to)
 
     def hop_c(i, kind):
         d = kind % 2
@@ -183,7 +193,7 @@
             src, dst = Q2[i].at[0, 1 - d, rel(i, C, AHEAD[d])], P2[i].at[d, 1 - d]
         else:
             src, dst = P1[i].at[d], P2[i].at[d, d]
-        return copy(src, dst, c_s.at[i, kind], c_r.at[i, kind], to)
+        return copy(src, dst, c_s.at[i, min(kind // 2, 1)], c_r.at[i, min(kind, 2)], to)
 
     def farthest(j):
         rb = order(j)
@@ -205,7 +215,7 @@
             for l in SIDES:
                 ref = at(i, l, a, b, c, k)
                 ref[...] = sum0(i, l, a, b, c).astype(BF16)
-                copy(ref, R1[i].at[l, b, c], a_s.at[i, l, 2], a_r.at[i, l, 2], near(AXES[i][0], AHEAD[l])).start()
+                copy(ref, R1[i].at[l, b, c], a_s.at[i, 0], a_r.at[i, l, 2], near(AXES[i][0], AHEAD[l])).start()
 
     loop(farthest_first)
     loop(farthest, start=1)
@@ -243,8 +253,7 @@
 
     def arrived_a(i, rb):
         traded(i, 0, rb)
-        for kind in LANDED:
-            hop_a(i, kind, rb).wait_recv()
+        landed(R1[i].at[0], a_r.at[i, 2, rb])
 
     def settle_a(i, l, rb, rc):
         b, c = rel(i, B, rb), rel(i, C, rc)
@@ -278,11 +287,14 @@
 
     loop(near_b)
     for i in EACH:
+        sent(R1[i], a_s.at[i, 0])
+        sent(R2[i], a_s.at[i, 1])
+        sent(at(i, ALL, ALL, ALL, ALL, k), d2d_s.at[i])
+    for i in EACH:
         arrived_a(i, 0)
 
     def arrived_b(i, rc):
-        for kind in LANDED:
-            hop_b(i, kind, rc).wait_recv()
+        landed(P2[i], b_r.at[i, 2, rc])
 
     for i in EACH:
         arrived_b(i, 2)
@@ -297,6 +309,9 @@
             Q2[i][0, 1 - d, c] = sum2(i, 1 - d, c).astype(BF16)
             hop_c(i, 2 + d).start()
     for i in EACH:
+        sent(Q1[i], b_s.at[i, 0])
+        sent(Q2[i], b_s.at[i, 1])
+    for i in EACH:
         for d in SIDES:
             hop_c(i, d).wait_recv()
             P1[i][d] = (f32(P1[i][d]) + sum2(i, d, rel(i, C, AHEAD[d]))).astype(BF16)
@@ -305,8 +320,7 @@
         arrived_b(i, 0)
     squares = jnp.zeros((8, 128), F32)
     for i in (2, 0, 1):
-        for kind in LANDED:
-            hop_c(i, kind).wait_recv()
+        landed(P2[i], c_r.at[i, 2])
         for l in SIDES:
             total = sum3(i, l).astype(BF16)
             if i == 2:
@@ -324,18 +338,9 @@
                 copy(quad_g.at[q], quad_g.at[q], x_s.at[n], x_r.at[n], quad[n]).start()
     norms[0, 0] = jnp.sum(squares, axis=0, keepdims=True)
 
-    def drain(j):
-        for i in EACH:
-            for kind in range(6):
-                hop_a(i, kind, j).wait_send()
-                hop_b(i, kind, j).wait_send()
-            for ra in PLACES:
-                trade(i, ra, j).wait_send()
-
-    loop(drain)
-    for i in EACH:
-        for kind in range(6):
-            hop_c(i, kind).wait_send()
+    for i in EACH:
+        sent(P1[i], c_s.at[i, 0])
+        sent(P2[i], c_s.at[i, 1])
 
     line, plane = lax.rem(me, 8), me // 8
     for turn, others in ((0, [plane * 8 + lax.rem(line + by, 8) for by in range(1, 8)]), (1, [lax.rem(plane + by, 16) * 8 + line for by in range(1, 16)])):
@@ -398,13 +403,11 @@
             ref = at(i, ALL, a, b, c, k)
         else:
             ref = at(i, d, a, b, rel(i, C, BEHIND[d]), k)
-        return copy(ref, ref, c_s.at[i, kind], c_r.at[i, kind], near(AXES[i][2], AHEAD[d]))
-
-    def came_c(i, kind):
-        d = kind % 2
+        return copy(ref, ref, c_s.at[i, 1 - kind // 2], c_r.at[i, min(kind, 2)], near(AXES[i][2], AHEAD[d]))
+
+    def came_c(i, d):
         a, b, _ = home[i]
-        ref = at(i, ALL, a, b, rel(i, C, BEHIND[d]), k) if kind < 2 else at(i, d, a, b, rel(i, C, FAR), k)
-        copy(ref, ref, c_s.at[i, kind], c_r.at[i, kind], partner).wait_recv()
+        landed(at(i, ALL, a, b, rel(i, C, BEHIND[d]), k), c_r.at[i, d])
 
     def back_b(i, kind):
         d = kind % 2
@@ -413,12 +416,10 @@
             ref = at(i, ALL, a, b, ALL, k)
         else:
             ref = at(i, d, a, rel(i, B, BEHIND[d]), ALL, k)
-        return copy(ref, ref, b_s.at[i, kind, 0], b_r.at[i, kind, 0], near(AXES[i][1], AHEAD[d]))
-
-    def came_b(i, kind):
-        d = kind % 2
-        ref = at(i, ALL, home[i][0], rel(i, B, BEHIND[d]), ALL, k) if kind < 2 else at(i, d, home[i][0], rel(i, B, FAR), ALL, k)
-        copy(ref, ref, b_s.at[i, kind, 0], b_r.at[i, kind, 0], partner).wait_recv()
+        return copy(ref, ref, b_s.at[i, 1 - kind // 2], b_r.at[i, min(kind, 2), 0], near(AXES[i][1], AHEAD[d]))
+
+    def came_b(i, d):
+        landed(at(i, ALL, home[i][0], rel(i, B, BEHIND[d]), ALL, k), b_r.at[i, d, 0])
 
     def back_a(i, kind, rb):
         d, b = kind % 2, rel(i, B, rb)
@@ -426,28 +427,22 @@
             ref = at(i, ALL, home[i][0], b, ALL, k)
         else:
             ref = at(i, d, rel(i, A, BEHIND[d]), b, ALL, k)
-        return copy(ref, ref, a_s.at[i, kind, rb], a_r.at[i, kind, rb], near(AXES[i][0], AHEAD[d]))
-
-    def came_a(i, kind, rb):
-        d, b = kind % 2, rel(i, B, rb)
-        ref = at(i, ALL, rel(i, A, BEHIND[d]), b, ALL, k) if kind < 2 else at(i, d, rel(i, A, FAR), b, ALL, k)
-        copy(ref, ref, a_s.at[i, kind, rb], a_r.at[i, kind, rb], partner).wait_recv()
+        return copy(ref, ref, a_s.at[i, 1 - kind // 2], a_r.at[i, min(kind, 2), rb], near(AXES[i][0], AHEAD[d]))
+
+    def came_a(i, d, rb):
+        landed(at(i, ALL, rel(i, A, BEHIND[d]), rel(i, B, rb), ALL, k), a_r.at[i, d, rb])
 
     def share(i, ra, rb):
         ref = at(i, ALL, rel(i, A, ra), rel(i, B, rb), ALL, k)
-        return copy(ref, ref, d2d_s.at[i, ra, rb], d2d_r.at[i, ra, rb], partner)
-
-    def shared(i, ra, rb):
-        ref = at(i, ALL, rel(i, A, ra), rel(i, B, rb), ALL, 1 - k)
-        copy(ref, ref, d2d_s.at[i, ra, rb], d2d_r.at[i, ra, rb], partner).wait_recv()
+        return copy(ref, ref, d2d_s.at[i], share_r.at[i], partner)
 
     def spread(i, c):
         a, b, _ = home[i]
         ref = at(i, ALL, a, b, c, k)
         for d in SIDES:
-            copy(ref, ref, b_s.at[i, d, 0], b_r.at[i, d, 0], near(AXES[i][1], AHEAD[d])).start()
-        for d in SIDES:
-            copy(ref, ref, a_s.at[i, d, 0], a_r.at[i, d, 0], near(AXES[i][0], AHEAD[d])).start()
+            copy(ref, ref, b_s.at[i, 1], b_r.at[i, d, 0], near(AXES[i][1], AHEAD[d])).start()
+        for d in SIDES:
+            copy(ref, ref, a_s.at[i, 1], a_r.at[i, d, 0], near(AXES[i][0], AHEAD[d])).start()
 
     def begin(i):
         for kind in SIDES:
@@ -472,8 +467,7 @@
         for d in SIDES:
             spread(i, rel(i, C, AHEAD[d]))
     for i in EACH:
-        for d in SIDES:
-            came_c(i, 2 + d)
+        landed(P1[i], c_r.at[i, 2])
         spread(i, rel(i, C, FAR))
         share(i, 0, 0).start()
     for i in EACH:
@@ -486,8 +480,7 @@
                 back_a(i, kind, rb).start()
             share(i, 0, rb).start()
     for i in EACH:
-        for d in SIDES:
-            came_b(i, 2 + d)
+        landed(Q1[i], b_r.at[i, 2, 0])
         for kind in SIDES:
             back_a(i, kind, 2).start()
         share(i, 0, 2).start()
@@ -504,7 +497,7 @@
 
     def tail(i, d, c):
         ref = at(i, d, rel(i, A, BEHIND[d]), rel(i, B, FAR), c, k)
-        return copy(ref, ref, a_s.at[i, 2 + d, 2], tail_r.at[i, d, c], near(AXES[i][0], AHEAD[d]))
+        return copy(ref, ref, a_s.at[i, 0], tail_r.at[i, c], near(AXES[i][0], AHEAD[d]))
 
     for i in EACH:
         for d in SIDES:
@@ -523,35 +516,29 @@
     def last(j):
         rb = lax.rem(order(j) + 2, 4)
         for i in EACH:
-            for d in SIDES:
-                came_a(i, 2 + d, rb)
+            landed(Q1[i], a_r.at[i, 2, rb])
             share(i, 2, rb).start()
 
     loop(last, 3)
 
     def last_tail(c):
         for i in EACH:
-            for d in SIDES:
-                ref = at(i, d, rel(i, A, FAR), rel(i, B, FAR), c, k)
-                copy(ref, ref, a_s.at[i, 2 + d, 2], tail_r.at[i, d, c], partner).wait_recv()
+            landed(P1[i], tail_r.at[i, c])
             ref = at(i, ALL, rel(i, A, FAR), rel(i, B, FAR), c, k)
-            copy(ref, ref, d2d_s.at[i, 2, 2], d2d_r.at[i, 2, 2], partner).start()
+            copy(ref, ref, d2d_s.at[i], share_r.at[i], partner).start()
 
     loop(last_tail)
 
-    def finish(j):
-        for i in EACH:
-            for ra in PLACES:
-                shared(i, ra, j)
-                share(i, ra, j).wait_send()
-            for kind in PLACES:
-                back_a(i, kind, j).wait_send()
-
-    loop(finish)
-    for i in EACH:
-        for kind in PLACES:
-            back_b(i, kind).wait_send()
-            back_c(i, kind).wait_send()
+    for i in EACH:
+        sent(R1[i], a_s.at[i, 0])
+        sent(R2[i], a_s.at[i, 1])
+        sent(Q1[i], b_s.at[i, 0])
+        sent(Q2[i], b_s.at[i, 1])
+        sent(P1[i], c_s.at[i, 0])
+        sent(P2[i], c_s.at[i, 1])
+    for i in EACH:
+        landed(at(i, ALL, ALL, ALL, ALL, 1 - k), share_r.at[i])
+        sent(at(i, ALL, ALL, ALL, ALL, k), d2d_s.at[i])
 
 
 def write_wide(n_wide, *refs):
@@ -617,9 +604,9 @@
                 pltpu.VMEM((LAYERS, n_rows, tall), BF16),
                 pltpu.VMEM((4, LAYERS, n_rows, quarter), BF16),
                 pltpu.VMEM((2, 16, 1, 128), F32),
-                dma((3, 4, 4)), dma((9,)), dma((3, 4, 4)), dma((3, 4, 4)),
-                dma((3, 6, 4)), dma((3, 6, 4)), dma((3, 6, 4)), dma((3, 6, 4)), dma((3, 6)), dma((3, 6)),
-                dma((6,)), dma((6,)), dma((2, 16)), dma((2, 16)), dma((3, 4)), dma((3, 4)), dma((3, 2, 4)),
+                dma((3, 4, 4)), dma((9,)), dma((3,)), dma((3, 4, 4)),
+                dma((3, 2)), dma((3, 3, 4)), dma((3, 2)), dma((3, 3, 4)), dma((3, 2)), dma((3, 3)),
+                dma((6,)), dma((6,)), dma((2, 16)), dma((2, 16)), dma((3, 4)), dma((3, 4)), dma((3, 4)), dma((3,)),
             ],
             compiler_params=pltpu.CompilerParams(collective_id=0, has_side_effects=True, vmem_limit_bytes=26600000),
             name="step",

time: 170 us -> 168 us (0.988)
  Pallas kernels: 169 us -> 167 us
    pallas_call x1, Pallas kernels: 157 us -> 154 us  [step(): pl.pallas_call(functools.partial(step_kernel, count), out_shape=blocks +...]
where the time goes in v4:
time: 168 us; the launch traced here: 167 us
  Pallas kernels  167 us (99%)
    pallas_call x1, Pallas kernels, step(): pl.pallas_call(functools.partial(step_kernel, count), out_shape=blocks +...  154 us
    pallas_call x2, Pallas kernels, write(): pl.pallas_call(kernel, out_shape=outs, in_specs=[vmem] * len(arrays), out...  12.6 us

profile of v4, /device:TPU:1, one launch (start us, length us, event | category | flops | bytes accessed | tf_op | source)
XLA Modules:
  0.0 167.4 jit_solution(2874558395535990816)
XLA Ops:
  0.6 154.1 %step.1 = (bf16[2,4,4,4,2,8,2816]{6,5,4,3,2,1,0:T(8,128)(2,1)S(1)}, bf16[2,4,4,4,2,8,2816]{6,5,4,3,2,1,0:T(8,128)(2,1)S(1)}, bf16[2,4,4,4,2,11,8,256]{7,6,5,4,3,...) custom-call(bf16[2,4,4,4,2,8,2816]{6,5,4,3,2,1,0:T(8,128)(2,1)} %bit, ...), custom_call_target="tpu_custom_call" | custom-call | tf_op jit(solution)/shard_map/step/pallas_call | solution.py:587
  154.8 7.9 %write.2 = (bf16[2,4,4,4,2,8,2816]{6,5,4,3,2,1,0:T(8,128)(2,1)}, bf16[2,4,4,4,2,8,2816]{6,5,4,3,2,1,0:T(8,128)(2,1)}) custom-call(bf16[2,4,4,4,2,8,2816]{6,5,4,3,2,1,0:T(8,128)(2,1)S(1)} %get-tuple-element.27.refs_0_, bf16[2,4,4,4,2,8,2816]{6,5,4,3,2,1,0:T(8,128)(2,1)S(1)} %get-tuple-element.28.refs_1_), custom_call_target="tpu_custom_call" | custom-call | tf_op jit(solution)/shard_map/write/pallas_call | solution.py:616
  162.7 4.8 %write.3 = (bf16[2,4,4,2,11,8,1024]{6,5,4,3,2,1,0:T(8,128)(2,1)}, f32[2,8,2816]{2,1,0:T(8,128)}, f32[2,8,2816]{2,1,0:T(8,128)}, f32[22,2,1024]{2,1,0:T(2,128)}, ...) custom-call(bf16[2,4,4,4,2,11,8,256]{7,6,5,4,3,2,1,0:T(8,128)(2,1)S(1)} %get-tuple-element.31.W, ...), custom_call_target="tpu_custom_call" | custom-call | tf_op jit(solution)/shard_map/write/pallas_call | solution.py:616

commit v5 on v4

--- a/solution.py
+++ b/solution.py
@@ -33,11 +33,12 @@
     count, gg, gu, gd, wg, wu, wd, mg, mu, md, vg, vu, vd,
     Wg, Wu, Wd, mg2, mu2, md2, vg2, vu2, vd2,
     R1g, R1u, R1d, R2g, R2u, R2d, Q1g, Q1u, Q1d, Q2g, Q2u, Q2d, P1g, P1u, P1d, P2g, P2u, P2d,
-    own_g, own_u, own_d, quad_g, rows, new_rows, cols, norms,
+    partial_g, partial_u, partial_d, own_g, own_u, own_d, quad_g, rows, new_rows, cols, norms,
     load_sem, own_sem, d2d_s, d2d_r, a_s, a_r, b_s, b_r, c_s, c_r, x_s, x_r, n_s, n_r, piece_l, piece_r, tail_r, share_r,
 ):
     g_in, W, w_in = (gg, gu, gd), (Wg, Wu, Wd), (wg, wu, wd)
     R1, R2, Q1, Q2, P1, P2 = (R1g, R1u, R1d), (R2g, R2u, R2d), (Q1g, Q1u, Q1d), (Q2g, Q2u, Q2d), (P1g, P1u, P1d), (P2g, P2u, P2d)
+    partial = (partial_g, partial_u, partial_d)
     quarter = cols.shape[-1]
     me = lax.axis_index("dp")
     k = lax.rem(me, 2)
@@ -159,9 +160,6 @@
     def sum2(i, l, c):
         return sum1(i, l, home[i][1], c) + f32(Q2[i][0, l, c]) + f32(Q2[i][1, l, c])
 
-    def sum3(i, l):
-        return sum2(i, l, home[i][2]) + f32(P2[i][0, l]) + f32(P2[i][1, l])
-
     def hop_a(i, kind, rb):
         d, b = kind % 2, rel(i, B, rb)
         to = near(AXES[i][0], AHEAD[d])
@@ -309,20 +307,25 @@
             Q2[i][0, 1 - d, c] = sum2(i, 1 - d, c).astype(BF16)
             hop_c(i, 2 + d).start()
     for i in EACH:
+        for d in SIDES:
+            partial[i][d] = sum2(i, d, rel(i, C, AHEAD[d]))
+    for i in EACH:
         sent(Q1[i], b_s.at[i, 0])
         sent(Q2[i], b_s.at[i, 1])
     for i in EACH:
         for d in SIDES:
             hop_c(i, d).wait_recv()
-            P1[i][d] = (f32(P1[i][d]) + sum2(i, d, rel(i, C, AHEAD[d]))).astype(BF16)
+            P1[i][d] = (f32(P1[i][d]) + partial[i][d]).astype(BF16)
             hop_c(i, 4 + d).start()
     for i in EACH:
         arrived_b(i, 0)
+        for l in SIDES:
+            partial[i][l] = sum2(i, l, home[i][2])
     squares = jnp.zeros((8, 128), F32)
     for i in (2, 0, 1):
         landed(P2[i], c_r.at[i, 2])
         for l in SIDES:
-            total = sum3(i, l).astype(BF16)
+            total = (partial[i][l] + f32(P2[i][0, l]) + f32(P2[i][1, l])).astype(BF16)
             if i == 2:
                 quad_g[q, l] = total
             else:
@@ -343,10 +346,25 @@
         sent(P2[i], c_s.at[i, 1])
 
     line, plane = lax.rem(me, 8), me // 8
+    def build_rows():
+        for one in own:
+            one.wait()
+        for n in EACH:
+            copy(quad_g.at[q], quad_g.at[q], x_s.at[n], x_r.at[n], quad[n]).wait_send()
+            theirs = quad_g.at[lax.rem(q + n + 1, 4)]
+            copy(theirs, theirs, x_s.at[2 - n], x_r.at[2 - n], quad[n]).wait_recv()
+        for l in SIDES:
+            for n in PLACES:
+                rows[0, l, :, n * quarter : (n + 1) * quarter] = f32(quad_g[n, l]).reshape(4 * n_rows, quarter)
+            rows[1, l] = f32(own_d[l]).reshape(4 * n_rows, 4 * quarter)
+
+    n_rows = md.shape[0]
     for turn, others in ((0, [plane * 8 + lax.rem(line + by, 8) for by in range(1, 8)]), (1, [lax.rem(plane + by, 16) * 8 + line for by in range(1, 16)])):
         hops = [copy(norms.at[turn, 0], norms.at[turn, by], n_s.at[turn, by], n_r.at[turn, by], to) for by, to in enumerate(others, 1)]
         for hop in hops:
             hop.start()
+        if turn == 1:
+            build_rows()
         for hop in hops:
             hop.wait()
         squares = jnp.sum(norms[turn, 0 : len(hops) + 1], axis=0)
@@ -361,40 +379,6 @@
         v = 0.95 * v + 0.05 * g * g
         step = m * lax.rsqrt(v + 1e-8) + 0.1 * w
         return (w - 0.02 * step).astype(BF16), m, v
-
-    for one in own:
-        one.wait()
-    for n in EACH:
-        copy(quad_g.at[q], quad_g.at[q], x_s.at[n], x_r.at[n], quad[n]).wait_send()
-        theirs = quad_g.at[lax.rem(q + n + 1, 4)]
-        copy(theirs, theirs, x_s.at[2 - n], x_r.at[2 - n], quad[n]).wait_recv()
-    n_rows = md.shape[0]
-    for l in SIDES:
-        for n in PLACES:
-            rows[0, :, n * quarter : (n + 1) * quarter] = f32(quad_g[n, l]).reshape(4 * n_rows, quarter)
-        rows[1] = f32(own_d[l]).reshape(4 * n_rows, 4 * quarter)
-        for n in PLACES:
-
-            @pl.when(q == n)
-            def _():
-                mine = slice(n * n_rows, (n + 1) * n_rows)
-                new, m, v = adamw(rows[1, mine, :], md2[:, l, :], vd2[:, l, :], rows[0, mine, :])
-                new_rows[l] = new
-                md2[:, l, :] = m
-                vd2[:, l, :] = v
-                cols[n, l] = new[:, n * quarter : (n + 1) * quarter]
-
-    def piece(n):
-        to = lax.rem(q + n + 1, 4)
-        return new_rows.at[:, :, pl.ds(pl.multiple_of(to * quarter, quarter), quarter)]
-
-    for n in EACH:
-        copy(piece(n), cols.at[q], x_s.at[3 + n], x_r.at[3 + n], quad[n]).start()
-
-    for i, own_w, m_ref, v_ref in ((0, own_g, mg2, vg2), (1, own_u, mu2, vu2)):
-        for l in SIDES:
-            new, m_ref[l], v_ref[l] = adamw(f32(own_w[l]), m_ref[l], v_ref[l], f32(P2[i][0, l]))
-            at(i, l, *home[i], k)[...] = new
 
     def back_c(i, kind):
         d = kind % 2
@@ -449,16 +433,38 @@
             back_c(i, kind).start()
         spread(i, home[i][2])
 
-    begin(0)
-    begin(1)
+    for i, own_w, m_ref, v_ref in ((0, own_g, mg2, vg2), (1, own_u, mu2, vu2)):
+        for l in SIDES:
+            new, m_ref[l], v_ref[l] = adamw(f32(own_w[l]), m_ref[l], v_ref[l], f32(P2[i][0, l]))
+            at(i, l, *home[i], k)[...] = new
+        begin(i)
+
+    for l in SIDES:
+        for n in PLACES:
+
+            @pl.when(q == n)
+            def _():
+                mine = slice(n * n_rows, (n + 1) * n_rows)
+                new, m, v = adamw(rows[1, l, mine, :], md2[:, l, :], vd2[:, l, :], rows[0, l, mine, :])
+                new_rows[l] = new
+                md2[:, l, :] = m
+                vd2[:, l, :] = v
+                cols[n, l] = new[:, n * quarter : (n + 1) * quarter]
+
+    def piece(n):
+        to = lax.rem(q + n + 1, 4)
+        return new_rows.at[:, :, pl.ds(pl.multiple_of(to * quarter, quarter), quarter)]
+
+    for n in EACH:
+        copy(piece(n), cols.at[q], x_s.at[3 + n], x_r.at[3 + n], quad[n]).start()
     for n in EACH:
         copy(piece(n), cols.at[q], x_s.at[3 + n], x_r.at[3 + n], quad[n]).wait_send()
         theirs = cols.at[lax.rem(q + n + 1, 4)]
         copy(theirs, theirs, x_s.at[5 - n], x_r.at[5 - n], quad[n]).wait_recv()
     for l in SIDES:
         for n in PLACES:
-            rows[0, n * n_rows : (n + 1) * n_rows, 0:quarter] = f32(cols[n, l])
-        at(2, l, *home[2], k)[...] = rows[0, :, 0:quarter].reshape(n_rows // 2, 8, quarter).astype(BF16)
+            rows[0, l, n * n_rows : (n + 1) * n_rows, 0:quarter] = f32(cols[n, l])
+        at(2, l, *home[2], k)[...] = rows[0, l, :, 0:quarter].reshape(n_rows // 2, 8, quarter).astype(BF16)
     begin(2)
     for i in EACH:
         for d in SIDES:
@@ -596,11 +602,12 @@
                 *[pltpu.VMEM((2, LAYERS, 4, *u), BF16) for u in units],
                 *[pltpu.VMEM((2, *u), BF16) for u in units],
                 *[pltpu.VMEM((2, LAYERS, *u), BF16) for u in units],
+                *[pltpu.VMEM((LAYERS, *u), F32) for u in units],
                 pltpu.VMEM((LAYERS, 8, wide), BF16),
                 pltpu.VMEM((LAYERS, 8, wide), BF16),
                 pltpu.VMEM((LAYERS, n_rows // 2, 8, tall), BF16),
                 pltpu.VMEM((4, LAYERS, *units[2]), BF16),
-                pltpu.VMEM((2, 4 * n_rows, tall), F32),
+                pltpu.VMEM((2, LAYERS, 4 * n_rows, tall), F32),
                 pltpu.VMEM((LAYERS, n_rows, tall), BF16),
                 pltpu.VMEM((4, LAYERS, n_rows, quarter), BF16),
                 pltpu.VMEM((2, 16, 1, 128), F32),

time: 168 us -> 169 us (level)
  no operation moved by 1% of the time
where the time goes in v5:
time: 169 us
  Pallas kernels  168 us (99%)
    pallas_call x1, Pallas kernels, step(): pl.pallas_call(functools.partial(step_kernel, count), out_shape=blocks +...  155 us
    pallas_call x2, Pallas kernels, write(): pl.pallas_call(kernel, out_shape=outs, in_specs=[vmem] * len(arrays), out...  12.6 us

profile of v5, /device:TPU:1, one launch (start us, length us, event | category | flops | bytes accessed | tf_op | source)
XLA Modules:
  0.0 168.7 jit_solution(8499286200621058623)
XLA Ops:
  0.6 155.4 %step.1 = (bf16[2,4,4,4,2,8,2816]{6,5,4,3,2,1,0:T(8,128)(2,1)S(1)}, bf16[2,4,4,4,2,8,2816]{6,5,4,3,2,1,0:T(8,128)(2,1)S(1)}, bf16[2,4,4,4,2,11,8,256]{7,6,5,4,3,...) custom-call(bf16[2,4,4,4,2,8,2816]{6,5,4,3,2,1,0:T(8,128)(2,1)} %bit, ...), custom_call_target="tpu_custom_call" | custom-call | tf_op jit(solution)/shard_map/step/pallas_call | solution.py:593
  156.0 7.9 %write.2 = (bf16[2,4,4,4,2,8,2816]{6,5,4,3,2,1,0:T(8,128)(2,1)}, bf16[2,4,4,4,2,8,2816]{6,5,4,3,2,1,0:T(8,128)(2,1)}) custom-call(bf16[2,4,4,4,2,8,2816]{6,5,4,3,2,1,0:T(8,128)(2,1)S(1)} %get-tuple-element.27.refs_0_, bf16[2,4,4,4,2,8,2816]{6,5,4,3,2,1,0:T(8,128)(2,1)S(1)} %get-tuple-element.28.refs_1_), custom_call_target="tpu_custom_call" | custom-call | tf_op jit(solution)/shard_map/write/pallas_call | solution.py:623
  163.9 4.8 %write.3 = (bf16[2,4,4,2,11,8,1024]{6,5,4,3,2,1,0:T(8,128)(2,1)}, f32[2,8,2816]{2,1,0:T(8,128)}, f32[2,8,2816]{2,1,0:T(8,128)}, f32[22,2,1024]{2,1,0:T(2,128)}, ...) custom-call(bf16[2,4,4,4,2,11,8,256]{7,6,5,4,3,2,1,0:T(8,128)(2,1)S(1)} %get-tuple-element.31.W, ...), custom_call_target="tpu_custom_call" | custom-call | tf_op jit(solution)/shard_map/write/pallas_call | solution.py:623

commit v6 on v5

--- a/solution.py
+++ b/solution.py
@@ -433,12 +433,6 @@
             back_c(i, kind).start()
         spread(i, home[i][2])
 
-    for i, own_w, m_ref, v_ref in ((0, own_g, mg2, vg2), (1, own_u, mu2, vu2)):
-        for l in SIDES:
-            new, m_ref[l], v_ref[l] = adamw(f32(own_w[l]), m_ref[l], v_ref[l], f32(P2[i][0, l]))
-            at(i, l, *home[i], k)[...] = new
-        begin(i)
-
     for l in SIDES:
         for n in PLACES:
 
@@ -457,6 +451,12 @@
 
     for n in EACH:
         copy(piece(n), cols.at[q], x_s.at[3 + n], x_r.at[3 + n], quad[n]).start()
+    for i, own_w, m_ref, v_ref in ((0, own_g, mg2, vg2), (1, own_u, mu2, vu2)):
+        for l in SIDES:
+            new, m_ref[l], v_ref[l] = adamw(f32(own_w[l]), m_ref[l], v_ref[l], f32(P2[i][0, l]))
+            at(i, l, *home[i], k)[...] = new
+        begin(i)
+
     for n in EACH:
         copy(piece(n), cols.at[q], x_s.at[3 + n], x_r.at[3 + n], quad[n]).wait_send()
         theirs = cols.at[lax.rem(q + n + 1, 4)]

time: 169 us -> 167 us (0.988)
  Pallas kernels: 168 us -> 166 us
where the time goes in v6:
time: 167 us
  Pallas kernels  166 us (99%)
    pallas_call x1, Pallas kernels, step(): pl.pallas_call(functools.partial(step_kernel, count), out_shape=blocks +...  154 us
    pallas_call x2, Pallas kernels, write(): pl.pallas_call(kernel, out_shape=outs, in_specs=[vmem] * len(arrays), out...  12.6 us

profile of v6, /device:TPU:1, one launch (start us, length us, event | category | flops | bytes accessed | tf_op | source)
XLA Modules:
  0.0 167.1 jit_solution(9020616727479877445)
XLA Ops:
  0.6 153.8 %step.1 = (bf16[2,4,4,4,2,8,2816]{6,5,4,3,2,1,0:T(8,128)(2,1)S(1)}, bf16[2,4,4,4,2,8,2816]{6,5,4,3,2,1,0:T(8,128)(2,1)S(1)}, bf16[2,4,4,4,2,11,8,256]{7,6,5,4,3,...) custom-call(bf16[2,4,4,4,2,8,2816]{6,5,4,3,2,1,0:T(8,128)(2,1)} %bit, ...), custom_call_target="tpu_custom_call" | custom-call | tf_op jit(solution)/shard_map/step/pallas_call | solution.py:593
  154.5 7.9 %write.2 = (bf16[2,4,4,4,2,8,2816]{6,5,4,3,2,1,0:T(8,128)(2,1)}, bf16[2,4,4,4,2,8,2816]{6,5,4,3,2,1,0:T(8,128)(2,1)}) custom-call(bf16[2,4,4,4,2,8,2816]{6,5,4,3,2,1,0:T(8,128)(2,1)S(1)} %get-tuple-element.27.refs_0_, bf16[2,4,4,4,2,8,2816]{6,5,4,3,2,1,0:T(8,128)(2,1)S(1)} %get-tuple-element.28.refs_1_), custom_call_target="tpu_custom_call" | custom-call | tf_op jit(solution)/shard_map/write/pallas_call | solution.py:623
  162.3 4.8 %write.3 = (bf16[2,4,4,2,11,8,1024]{6,5,4,3,2,1,0:T(8,128)(2,1)}, f32[2,8,2816]{2,1,0:T(8,128)}, f32[2,8,2816]{2,1,0:T(8,128)}, f32[22,2,1024]{2,1,0:T(2,128)}, ...) custom-call(bf16[2,4,4,4,2,11,8,256]{7,6,5,4,3,2,1,0:T(8,128)(2,1)S(1)} %get-tuple-element.31.W, ...), custom_call_target="tpu_custom_call" | custom-call | tf_op jit(solution)/shard_map/write/pallas_call | solution.py:623
